TPU v7x, 128 devices: a whole 4x4x4 slice. The times are simulated.
128 devices in a mesh: seq: 64 (over y, z, x), fsdp: 2 (over core).
Axes of the slice: x: 4, y: 4, z: 4, core: 2. Of those that a mesh axis runs over, the one named last changes fastest.
Arguments:
- tokens: bfloat16 [2, 49152, 2560], P('fsdp', 'seq'), may hold values from -6 to 6
- bounds: int32 [2, 64, 2], P('fsdp', 'seq'), may hold values from 0 to 96, as said below
- in_weight: bfloat16 [2560, 5416], P(('seq', 'fsdp')), may hold values from -0.125 to 0.125
- conv_weight: float32 [4, 2816], replicated, may hold values from -0.6 to 0.6
- conv_bias: float32 [2816], replicated, may hold values from -3 to 3
- dt_bias: float32 [40], replicated, may hold values from -4 to 0
- decay_rate: float32 [40], replicated, may hold values from 1.2207031e-05 to 0.5
- skip_gain: float32 [40], replicated, may hold values from 0.1 to 1.9
- norm_gain: float32 [2560], replicated, may hold values from 0.1 to 1.9
Outputs:
- layer_out: bfloat16 [2, 49152, 2560], P('fsdp', 'seq')
Inputs may be any that keep to these rules, and one draw needn't show every extreme that they name: For sequence b, bounds[b, s] holds the first and one past the last block of the shard of index s of seq; shards are consecutive in s and cover all 96 blocks; each holds 1 to 3 blocks, and some shard holds 3.
All inputs are finite; a program needn't handle non-finite values.
Results may differ from a plain program's by a relative error of at most 0.0028.
The roundings to bfloat16 on the way count: a program that leaves them out, or rounds other values in their place, can miss the bound.
Values may be sent and summed in bfloat16 or wider, within the bound.
No kernel may reach another device: no remote copies, remote signals or barrier semaphores. Data moves between devices by JAX's collectives and lax.ppermute only.
A program may use at most 192 MiB of HBM per device.

v0:
```python
import jax
import jax.numpy as jnp
from jax import lax
from jax.sharding import Mesh
from jax.sharding import PartitionSpec as P

BLOCK = 256
SEQ_FSDP = ("seq_0", "seq_1", "seq_2", "fsdp")
SEQ = ("seq_0", "seq_1", "seq_2")


def passed_along(value, axis, steps):
    count = lax.axis_size(axis)
    leading, last = (max(0, -steps), min(count, count - steps))
    return lax.ppermute(value, axis, [(source, source + steps) for source in range(leading, last)])


def filled_with(shard, identity):
    return jax.tree.map(
        lambda part, zero: jnp.zeros_like(part) + jnp.asarray(zero, part.dtype), shard, identity
    )


def prefix_by_axis(shard, axes, combine, identity):
    before = start = filled_with(shard, identity)
    total = shard
    for axis in reversed(axes):
        length, place = (lax.axis_size(axis), lax.axis_index(axis))
        pieces = jax.tree.map(lambda part: lax.all_gather(part, axis), total)
        inside, total = (start, start)
        for k in range(length):
            passed = k < place
            total = combine(total, jax.tree.map(lambda part: part[k], pieces))
            inside = jax.tree.map(lambda new, old: jnp.where(passed, new, old), total, inside)
        before = combine(inside, before)
    return before


def block_terms(head_input, input_map, output_map, step_size, decay_rate):
    log_decay = -(step_size * decay_rate[None, :]).T
    cumulative = jnp.cumsum(log_decay, axis=1)
    pairwise = cumulative[:, :, None] - cumulative[:, None, :]
    length = cumulative.shape[1]
    causal = jnp.arange(length)[:, None] >= jnp.arange(length)[None, :]
    pair_decay = jnp.exp(jnp.where(causal[None], pairwise, -jnp.inf))
    scores = jnp.dot(output_map, input_map.T, preferred_element_type=jnp.float32)
    mixing = scores[None] * pair_decay * step_size.T[:, None, :]
    inner_out = jnp.einsum("hij,jhp->ihp", mixing, head_input, precision=lax.Precision.HIGH)
    to_end = jnp.exp(cumulative[:, -1:] - cumulative) * step_size.T
    local_state = jnp.einsum(
        "hj,jhp,jn->hpn",
        to_end,
        head_input,
        input_map.astype(jnp.float32),
        precision=lax.Precision.HIGH,
    )
    return (inner_out, cumulative, local_state)


def carried(output_map, cumulative, state):
    reach = jnp.einsum(
        "in,hpn->ihp", output_map.astype(jnp.float32), state, precision=lax.Precision.HIGH
    )
    return jnp.exp(cumulative).T[:, :, None] * reach


def compose(earlier, later):
    return (earlier[0] * later[0], later[0][:, None, None] * earlier[1] + later[1])


def local(
    tokens, bounds, in_weight, conv_weight, conv_bias, dt_bias, decay_rate, skip_gain, norm_gain
):
    slots = tokens.shape[1]
    inner = norm_gain.shape[0]
    state_width = (conv_bias.shape[0] - inner) // 2
    heads = decay_rate.shape[0]
    head_dim = inner // heads
    kernel = conv_weight.shape[0]
    capacity = slots // BLOCK
    shard_blocks = bounds[0, 0, 1] - bounds[0, 0, 0]
    own_rows = tokens[0]
    summed = jnp.dot(
        own_rows,
        lax.all_gather(in_weight, SEQ_FSDP, axis=0, tiled=True),
        preferred_element_type=jnp.float32,
    )
    projected = summed.astype(jnp.bfloat16)
    gate = projected[:, :inner].astype(jnp.float32)
    mixed_in = projected[:, inner : 2 * inner + 2 * state_width]
    raw_step = projected[:, 2 * inner + 2 * state_width :].astype(jnp.float32)
    edge_rows = lax.dynamic_slice_in_dim(
        mixed_in, shard_blocks * BLOCK - (kernel - 1), kernel - 1, 0
    )
    previous = passed_along(edge_rows, SEQ, 1)
    extended = jnp.concatenate([previous, mixed_in], axis=0)
    convolved = jnp.zeros((slots, mixed_in.shape[1]), jnp.float32) + conv_bias[None, :]
    for offset in range(kernel):
        convolved = convolved + conv_weight[offset][None, :] * extended[
            offset : offset + slots
        ].astype(jnp.float32)
    conv_out = jax.nn.silu(convolved).astype(jnp.bfloat16)
    live_mask = jnp.arange(slots)[:, None] < shard_blocks * BLOCK
    step_size = jnp.where(live_mask, jax.nn.softplus(raw_step + dt_bias[None, :]), 0.0)
    pieces = []
    decay_total = jnp.ones((heads,), jnp.float32)
    summary_state = jnp.zeros((heads, head_dim, state_width), jnp.float32)
    for place in range(capacity):
        lower = place * BLOCK
        upper = lower + BLOCK
        in_values = (
            conv_out[lower:upper, :inner].astype(jnp.float32).reshape(BLOCK, heads, head_dim)
        )
        in_map = conv_out[lower:upper, inner : inner + state_width]
        out_map = conv_out[lower:upper, inner + state_width :]
        inner_out, cumulative, local_state = block_terms(
            in_values, in_map, out_map, step_size[lower:upper], decay_rate
        )
        block_decay = jnp.exp(cumulative[:, -1])
        summary_state = block_decay[:, None, None] * summary_state + local_state
        decay_total = decay_total * block_decay
        pieces.append((in_values, out_map, inner_out, cumulative, local_state, block_decay))
    identity = (
        jnp.ones((heads,), jnp.float32),
        jnp.zeros((heads, head_dim, state_width), jnp.float32),
    )
    incoming = prefix_by_axis((decay_total, summary_state), SEQ, compose, identity)
    state = incoming[1]
    results = []
    for in_values, out_map, inner_out, cumulative, local_state, block_decay in pieces:
        result = (
            inner_out + carried(out_map, cumulative, state) + skip_gain[None, :, None] * in_values
        )
        results.append(result.reshape(BLOCK, inner))
        state = block_decay[:, None, None] * state + local_state
    scanned = jnp.concatenate(results, axis=0)
    gated = scanned * jax.nn.silu(gate)
    normed = (
        gated
        * lax.rsqrt(jnp.mean(gated * gated, axis=1, keepdims=True) + 1e-05)
        * norm_gain[None, :]
    )
    layer_out = jnp.where(live_mask, normed, 0.0).astype(jnp.bfloat16)
    return layer_out[None]


def solution(mesh):
    split = Mesh(
        mesh.devices.reshape(4, 4, 4, mesh.shape["fsdp"]), ("seq_0", "seq_1", "seq_2", "fsdp")
    )
    return jax.shard_map(
        local,
        mesh=split,
        in_specs=(
            P("fsdp", SEQ, None),
            P("fsdp", SEQ, None),
            P(SEQ_FSDP, None),
            P(),
            P(),
            P(),
            P(),
            P(),
            P(),
        ),
        out_specs=P("fsdp", SEQ, None),
        check_vma=False,
    )
```

profile of v0, /device:TPU:0, one launch (start us, length us, event | category | flops | bytes accessed | tf_op | source)
XLA Modules:
  0.0 451.7 jit_solution(928340942018903259)
XLA Ops:
  6.5 0.7 all-gather.16.cloned.1.call-update
  7.3 1.4 fusion.109
  10.0 1.1 slice_reduce_fusion.9
  11.1 108.2 %all-gather.16.cloned.1.call-done = bf16[128,20,5416]{2,1,0:T(8,128)(2,1)} async-done(((bf16[1,20,5416]{2,1,0:T(8,128)(2,1)}), bf16[128,20,5416]{2,1,0:T(8,128)(2,1)}) %all-gather.16.cloned.1.call-update) | async-done | bytes 27729936 | tf_op jit(solution)/shard_map/all_gather | solution.py:85
  119.3 36.9 %reshape.339 = bf16[2560,5416]{1,0:T(8,128)(2,1)} reshape(bf16[128,20,5416]{2,1,0:T(8,128)(2,1)} %all-gather.16.cloned.1.call-done) | data formatting | bytes 55459840
  156.1 29.0 %convolution_convert_fusion = bf16[768,5416]{0,1:T(8,128)(2,1)} fusion(bf16[2560,5416]{1,0:T(8,128)(2,1)} %reshape.339, bf16[1,768,2560]{2,1,0:T(8,128)(2,1)} %param.9), kind=kOutput, calls=%fused_computation.18 | convolution fusion | flops 21300738048 | bytes 39981056 | tf_op jit(solution)/shard_map/dot_general | solution.py:83
  185.1 2.5 slice.251
  187.7 2.0 copy-done
  190.2 3.5 collective-permute-start
  193.8 1.0 fusion.78
  194.8 0.7 slice_bitcast_fusion.6
  195.5 0.6 reduce-window.26
  196.3 0.6 reduce-window.24
  197.2 0.6 reduce-window.20
  198.4 0.8 multiply_bitcast_fusion
  199.2 0.5 fusion.108
  199.7 0.4 copy.37
  200.1 16.0 %multiply_convert_fusion = bf16[768,2816]{0,1:T(8,128)(2,1)S(1)} fusion(bf16[768,2816]{0,1:T(8,128)(2,1)} %copy-done, bf16[3,2816]{0,1:T(8,128)(2,1)S(1)} %copy.37, f32[2816]{0:T(1024)S(1)} %get-tuple-element.7, f32[2816]{0:T(1024)S(1)} %get-tuple-element.8, f32[2816]{0:T(1024)S(1)} %get-tuple-element.6, f32[2816]{0:T(1024)S(1)} %get-tuple-element.5, ...), kind=kLoop, calls=%fused_computation.21 | loop fusion | flops 56229888 | bytes 8723968 | tf_op jit(solution)/shard_map/convert_element_type | solution.py:102
  216.5 0.9 fusion.46
  217.3 0.9 fusion.44
  218.2 0.8 copy-done.1
  219.0 0.4 copy-done.6
  219.4 1.9 fusion.56
  221.5 0.6 dynamic-slice
  222.9 9.7 %all-reduce = f32[160]{0:T(256)S(1)} all-reduce(f32[160]{0:T(256)S(1)} %dynamic-update-slice), channel_id=2, replica_groups=mesh['seq_0'=4,'seq_1'=4,'seq_2'=4,'fsdp'=2] {'seq_2'}, use_global_device_ids=true, to_apply=%add | all-reduce | flops 160 | bytes 1280
  232.7 10.3 %all-gather.3 = f32[4,1,40]{2,1,0:T(1,128)S(1)} all-gather(f32[1,1,40]{2,1,0:T(1,128)S(1)} %get-tuple-element.46), channel_id=1, replica_groups=mesh['seq_0'=4,'seq_1'=4,'seq_2'=4,'fsdp'=2] {'seq_1'}, dimensions={0}, use_global_device_ids=true | all-gather | bytes 800 | tf_op jit(solution)/shard_map/all_gather | solution.py:29
  243.0 0.6 fusion.101
  243.6 35.1 %all-gather.14.cloned.1.call-done = f32[160,64,128]{2,1,0:T(8,128)} async-done(((f32[40,64,128]{2,1,0:T(8,128)}), f32[160,64,128]{2,1,0:T(8,128)}) %all-gather.14.cloned.1.call-update) | async-done | bytes 5242896 | tf_op jit(solution)/shard_map/all_gather | solution.py:29
  278.6 4.0 bitcast_add_fusion.7
  282.7 57.7 %all-gather.10.cloned.1.call-done = f32[4,40,64,128]{3,2,1,0:T(8,128)} async-done(((f32[1,40,64,128]{3,2,1,0:T(8,128)}), f32[4,40,64,128]{3,2,1,0:T(8,128)}) %all-gather.10.cloned.1.call-update) | async-done | bytes 5242896 | tf_op jit(solution)/shard_map/all_gather | solution.py:29
  340.4 4.0 multiply_add_fusion.1
  344.4 0.6 iota_compare_fusion
  345.1 9.7 %all-gather.4 = f32[4,1,40]{2,1,0:T(1,128)S(1)} all-gather(f32[1,1,40]{2,1,0:T(1,128)S(1)} %get-tuple-element.39), channel_id=1, replica_groups=mesh['seq_0'=4,'seq_1'=4,'seq_2'=4,'fsdp'=2] {'seq_0'}, dimensions={0}, use_global_device_ids=true | all-gather | bytes 800 | tf_op jit(solution)/shard_map/all_gather | solution.py:29
  354.8 0.6 slice_bitcast_fusion.9
  355.4 1.1 fusion.87
  356.5 1.1 fusion.90
  357.6 1.1 fusion.97
  358.7 43.2 %all-gather.12.cloned.1.call-done = f32[4,40,64,128]{3,2,1,0:T(8,128)} async-done(((f32[1,40,64,128]{3,2,1,0:T(8,128)}), f32[4,40,64,128]{3,2,1,0:T(8,128)}) %all-gather.12.cloned.1.call-update) | async-done | bytes 5242896 | tf_op jit(solution)/shard_map/all_gather | solution.py:29
  401.9 8.0 %fusion.60 = f32[40,64,128]{2,1,0:T(8,128)S(1)} fusion(f32[4,40,64,128]{3,2,1,0:T(8,128)} %all-gather.12.cloned.1.call-done, f32[4,40,64,128]{3,2,1,0:T(8,128)} %all-gather.10.cloned.1.call-done, f32[160,64,128]{2,1,0:T(8,128)} %all-gather.14.cloned.1.call-done, f32[40]{0:T(128)} %copy-done.17, f32[40]{0:T(128)S(1)} %get-tuple-element.47, f32[40]{0:T(128)} %copy-done.18, ...), kind=kLoop, calls=%fused_computation.75 | loop fusion | flops 12124160 | bytes 17041612 | tf_op jit(solution)/shard_map/add | solution.py:68
  409.9 1.7 fusion.70
  411.7 1.7 fusion.77
  413.4 1.8 fusion.84
  415.3 5.2 %fusion.49 = f32[256,40,64]{0,2,1:T(8,128)S(1)} fusion(bf16[256,40,64]{0,2,1:T(8,128)(2,1)S(1)} %bitcast.222, f32[256,40,64]{0,2,1:T(8,128)S(1)} %fusion.70, f32[40,256]{1,0:T(8,128)S(1)} %copy-done.14, f32[40,256]{1,0:T(8,128)S(1)} %copy_bitcast_fusion, f32[256,256]{1,0:T(8,128)S(1)} %fusion.87, pred[256,256]{1,0:T(8,128)(4,1)S(1)} %copy-done.8, ...), kind=kOutput, calls=%fused_computation.66 | convolution fusion | flops 1020395520 | bytes 7004320 | tf_op jit(solution)/shard_map/hij,jhp->ihp/dot_general | solution.py:48
  420.6 5.5 %fusion.47 = f32[256,40,64]{0,2,1:T(8,128)S(1)} fusion(bf16[256,40,64]{0,2,1:T(8,128)(2,1)S(1)} %bitcast.220, f32[256,40,64]{0,2,1:T(8,128)S(1)} %fusion.77, f32[40,256]{1,0:T(8,128)S(1)} %copy-done.13, f32[40,256]{1,0:T(8,128)S(1)} %copy_bitcast_fusion.1, f32[256,256]{1,0:T(8,128)S(1)} %fusion.90, pred[256,256]{1,0:T(8,128)(4,1)S(1)} %copy-done.8, ...), kind=kOutput, calls=%fused_computation.64 | convolution fusion | flops 1020395520 | bytes 7004320 | tf_op jit(solution)/shard_map/hij,jhp->ihp/dot_general | solution.py:48
  426.1 5.2 %fusion.45 = f32[256,40,64]{0,2,1:T(8,128)S(1)} fusion(bf16[256,40,64]{0,2,1:T(8,128)(2,1)S(1)} %bitcast.218, f32[256,40,64]{0,2,1:T(8,128)S(1)} %fusion.84, f32[40,256]{1,0:T(8,128)S(1)} %copy-done.12, f32[40,256]{1,0:T(8,128)S(1)} %copy_bitcast_fusion.2, f32[256,256]{1,0:T(8,128)S(1)} %fusion.97, pred[256,256]{1,0:T(8,128)(4,1)S(1)} %copy-done.8, ...), kind=kOutput, calls=%fused_computation.62 | convolution fusion | flops 1020395520 | bytes 7004320 | tf_op jit(solution)/shard_map/hij,jhp->ihp/dot_general | solution.py:48
  431.3 4.4 multiply_reduce_fusion
  435.8 2.6 fusion.42
  438.4 6.3 %copy.50 = bf16[1,768,2560]{2,1,0:T(8,128)(2,1)} copy(bf16[1,768,2560]{1,2,0:T(8,128)(2,1)} %fusion.42) | data formatting | bytes 7864320 | tf_op jit(solution)/shard_map/broadcast_in_dim | solution.py:144
  (87 shorter events, 2.6 us)
Async XLA Ops:
  6.5 112.7 %all-gather.16.cloned.1.call-start = ((), (), s32[]{:S(2)}) async-start(), calls=%async_computation.3 | async-start | bytes 34080768 | tf_op jit(solution)/shard_map/all_gather | solution.py:85
  7.3 271.4 %all-gather.14.cloned.1.call-start = ((), (), s32[]{:S(2)}) async-start(), calls=%async_computation.2 | async-start | bytes 6553600 | tf_op jit(solution)/shard_map/all_gather | solution.py:29
  10.0 183.8 %copy-start.19 = (pred[768]{0:T(1024)(128)(4,1)}, pred[768]{0:T(1024)(128)(4,1)S(1)}, u32[]{:S(2)}) copy-start(pred[768]{0:T(1024)(128)(4,1)S(1)} %iota_compare_fusion.1) | copy-start | bytes 2308
  185.1 8.7 %copy-start.24 = (f32[40]{0:T(128)S(1)}, f32[40]{0:T(128)}, u32[]{:S(2)}) copy-start(f32[40]{0:T(128)} %param.14) | copy-start | bytes 484
  185.1 9.7 %copy-start.25 = (f32[40]{0:T(128)S(1)}, f32[40]{0:T(128)}, u32[]{:S(2)}) copy-start(f32[40]{0:T(128)} %param.15) | copy-start | bytes 484
  187.7 2.0 copy-start
  189.7 10.5 %copy-start.15 = (f32[2816]{0:T(1024)S(1)}, f32[2816]{0:T(1024)}, u32[]{:S(2)}) copy-start(f32[2816]{0:T(1024)} %param.13) | copy-start | bytes 33796
  190.2 9.5 %collective-permute-start = (bf16[3,2816]{1,0:T(4,128)(2,1)S(1)}, bf16[3,2816]{1,0:T(4,128)(2,1)S(1)}, u32[]{:S(2)}, u32[]{:S(2)}) collective-permute-start(bf16[3,2816]{1,0:T(4,128)(2,1)S(1)} %copy.36), channel_id=1, source_target_pairs={{0,2},{2,4},{4,6},{6,8},{8,10},{10,12},{12,14},{14,16},{16,18},{18... | collective-permute-start | bytes 50696 | tf_op jit(solution)/shard_map/ppermute | solution.py:15
  199.7 18.5 %copy-start.22 = (f32[40]{0:T(128)}, f32[40]{0:T(128)S(1)}, u32[]{:S(2)}) copy-start(f32[40]{0:T(128)S(1)} %exp.98) | copy-start | bytes 484
  216.2 2.9 copy-start.1
  216.4 1.8 copy-start.2
  216.4 1.8 copy-start.4
  216.5 3.0 copy-start.6
  219.4 2.0 copy-start.27
  221.4 119.1 %all-gather.10.cloned.1.call-start = ((), (), s32[]{:S(2)}) async-start(), calls=%async_computation | async-start | bytes 6553600 | tf_op jit(solution)/shard_map/all_gather | solution.py:29
  243.6 39.1 %copy-start.17 = (f32[40]{0:T(128)}, f32[40]{0:T(128)S(1)}, u32[]{:S(2)}) copy-start(f32[40]{0:T(128)S(1)} %get-tuple-element.44) | copy-start | bytes 484
  243.6 39.1 %copy-start.18 = (f32[40]{0:T(128)}, f32[40]{0:T(128)S(1)}, u32[]{:S(2)}) copy-start(f32[40]{0:T(128)S(1)} %get-tuple-element.45) | copy-start | bytes 484
  282.6 119.2 %all-gather.12.cloned.1.call-start = ((), (), s32[]{:S(2)}) async-start(), calls=%async_computation.1 | async-start | bytes 6553600 | tf_op jit(solution)/shard_map/all_gather | solution.py:29
  401.9 8.0 %copy-start.21 = (f32[40]{0:T(128)S(1)}, f32[40]{0:T(128)}, u32[]{:S(2)}) copy-start(f32[40]{0:T(128)} %get-tuple-element.49) | copy-start | bytes 484
  401.9 8.0 %copy-start.23 = (f32[40]{0:T(128)S(1)}, f32[40]{0:T(128)}, u32[]{:S(2)}) copy-start(f32[40]{0:T(128)} %copy-done.22) | copy-start | bytes 484
  413.4 1.8 copy-start.7
  413.4 1.8 copy-start.8
  413.4 1.8 copy-start.11
  413.4 1.8 copy-start.14
  413.4 1.8 copy-start.26
  415.3 5.3 %copy-start.5 = (bf16[256,2560]{0,1:T(8,128)(2,1)S(1)}, bf16[256,2560]{0,1:T(8,128)(2,1)}, u32[]{:S(2)}) copy-start(bf16[256,2560]{0,1:T(8,128)(2,1)} %copy-done.4) | copy-start | bytes 3932164
  415.3 5.2 %copy-start.10 = (f32[256,40]{0,1:T(8,128)S(1)}, f32[256,40]{0,1:T(8,128)}, u32[]{:S(2)}) copy-start(f32[256,40]{0,1:T(8,128)} %get-tuple-element.33) | copy-start | bytes 122884
  415.3 5.2 %copy-start.13 = (f32[40,256]{1,0:T(8,128)S(1)}, f32[40,256]{1,0:T(8,128)}, u32[]{:S(2)}) copy-start(f32[40,256]{1,0:T(8,128)} %get-tuple-element.24) | copy-start | bytes 122884
  420.5 5.5 %copy-start.3 = (bf16[256,2560]{0,1:T(8,128)(2,1)S(1)}, bf16[256,2560]{0,1:T(8,128)(2,1)}, u32[]{:S(2)}) copy-start(bf16[256,2560]{0,1:T(8,128)(2,1)} %copy-done.2) | copy-start | bytes 3932164
  420.5 5.5 %copy-start.9 = (f32[256,40]{0,1:T(8,128)S(1)}, f32[256,40]{0,1:T(8,128)}, u32[]{:S(2)}) copy-start(f32[256,40]{0,1:T(8,128)} %get-tuple-element.32) | copy-start | bytes 122884
  420.6 5.5 %copy-start.12 = (f32[40,256]{1,0:T(8,128)S(1)}, f32[40,256]{1,0:T(8,128)}, u32[]{:S(2)}) copy-start(f32[40,256]{1,0:T(8,128)} %get-tuple-element.23) | copy-start | bytes 122884
  431.3 4.5 copy-start.16
  431.3 4.5 copy-start.20
Sparse Core Ops, SparseCore 0:
  10.3 108.9 all-gather.15
  221.5 57.0 all-gather.13
  282.8 57.6 all-gather.9
  344.6 57.2 all-gather.11
where the time goes:
time: 460 us; the launch traced here: 452 us
  waiting for transfers between devices  245 us (53%)
  matrix products  57 us (12%)
  local copies, waits for them, and re-layouts  54 us (12%)
  other arithmetic  46.4 us (10%)
  blocking collectives  29.7 us (6%)
  between operations  15.9 us (3%)
    all_gather x3, waiting for transfers between devices, prefix_by_axis(): pieces = jax.tree.map(lambda part: lax.all_gather(part, axis), total)  136 us
    all_gather x1, waiting for transfers between devices, local(): lax.all_gather(in_weight, SEQ_FSDP, axis=0, tiled=True)  108 us
    unnamed x60, local copies, waits for them, and re-layouts  41 us
    dot_general x1, matrix products, local(): jnp.dot(own_rows, lax.all_gather(in_weight, SEQ_FSDP, axis=0, tiled=True)...  29 us
    all_gather x2, blocking collectives, prefix_by_axis(): pieces = jax.tree.map(lambda part: lax.all_gather(part, axis), total)  20 us
    convert_element_type x1, other arithmetic, local(): conv_out = jax.nn.silu(convolved).astype(jnp.bfloat16)  16 us
    add x3, other arithmetic, compose(): later[0][:, None, None] * earlier[1] + later[1]  16 us
    dot_general x3, matrix products, block_terms(): jnp.einsum('hij,jhp->ihp', mixing, head_input, precision=lax.Precision.HIGH)  15.9 us
  transfers between devices with their start and end apart: 5, of which 4 were waited for; matrix products, arithmetic and copies ran while one was open for 3% of the time, Pallas kernels for 0%

commit v1 on v0

v1 whole, which is shorter than its diff:
```python
import jax
import jax.numpy as jnp
from jax import lax
from jax.experimental import pallas as pl
from jax.experimental.pallas import tpu as pltpu
from jax.sharding import Mesh
from jax.sharding import PartitionSpec as P

BLOCK = 256
EDGE = 8
SEQ_FSDP = ("seq_0", "seq_1", "seq_2", "fsdp")
SEQ = ("seq_0", "seq_1", "seq_2")
F32 = jnp.float32
BF16 = jnp.bfloat16


def passed_along(value, axis, steps):
    count = lax.axis_size(axis)
    leading, last = (max(0, -steps), min(count, count - steps))
    return lax.ppermute(value, axis, [(source, source + steps) for source in range(leading, last)])


def swapped(value):
    return lax.ppermute(value, "fsdp", [(0, 1), (1, 0)])


def block_terms(head_input, input_map, output_map, step_size, decay_rate):
    log_decay = -(step_size * decay_rate[None, :]).T
    cumulative = jnp.cumsum(log_decay, axis=1)
    pairwise = cumulative[:, :, None] - cumulative[:, None, :]
    length = cumulative.shape[1]
    causal = jnp.arange(length)[:, None] >= jnp.arange(length)[None, :]
    pair_decay = jnp.exp(jnp.where(causal[None], pairwise, -jnp.inf))
    scores = jnp.dot(output_map, input_map.T, preferred_element_type=jnp.float32)
    mixing = scores[None] * pair_decay * step_size.T[:, None, :]
    inner_out = jnp.einsum("hij,jhp->ihp", mixing, head_input, precision=lax.Precision.HIGH)
    to_end = jnp.exp(cumulative[:, -1:] - cumulative) * step_size.T
    local_state = jnp.einsum(
        "hj,jhp,jn->hpn",
        to_end,
        head_input,
        input_map.astype(jnp.float32),
        precision=lax.Precision.HIGH,
    )
    return (inner_out, cumulative, local_state)


def carried(output_map, cumulative, state):
    reach = jnp.einsum(
        "in,hpn->ihp", output_map.astype(jnp.float32), state, precision=lax.Precision.HIGH
    )
    return jnp.exp(cumulative).T[:, :, None] * reach


def prefix_kernel(count, rows, got_ref, out_ref):
    decays = jnp.exp(got_ref[:, rows, :]).T
    state = jnp.zeros((rows, got_ref.shape[2]), F32)
    for source in range(count):
        out_ref[source] = state
        if source < count - 1:
            factor = jnp.broadcast_to(decays[:rows, source : source + 1], state.shape)
            state = state * factor + got_ref[source, :rows, :]


def incoming_state(log_total, summary):
    heads, head_dim, width = summary.shape
    count = lax.axis_size(SEQ)
    rows = heads * head_dim // count
    per_row = jnp.repeat(log_total, head_dim).reshape(count, rows)
    parts = jnp.pad(per_row[:, None, :], ((0, 0), (0, 7), (0, width - rows)))
    payload = jnp.concatenate([summary.reshape(count, rows, width), parts], axis=1)
    got = lax.all_to_all(payload, SEQ, 0, 0, tiled=True)
    before = pl.pallas_call(
        lambda got_ref, out_ref: prefix_kernel(count, rows, got_ref, out_ref),
        out_shape=jax.ShapeDtypeStruct((count, rows, width), F32),
        cost_estimate=pl.CostEstimate(flops=8_000_000, bytes_accessed=1_500_000, transcendentals=0),
        name="prefix",
    )(got)
    back = lax.all_to_all(before, SEQ, 0, 0, tiled=True)
    return back.reshape(heads, head_dim, width)


def local(
    tokens, bounds, in_weight, conv_weight, conv_bias, dt_bias, decay_rate, skip_gain, norm_gain
):
    slots = tokens.shape[1]
    inner = norm_gain.shape[0]
    state_width = (conv_bias.shape[0] - inner) // 2
    heads = decay_rate.shape[0]
    head_dim = inner // heads
    kernel = conv_weight.shape[0]
    capacity = slots // BLOCK
    half = inner // 2
    core = lax.axis_index("fsdp")
    shard_blocks = bounds[0, 0, 1] - bounds[0, 0, 0]
    own_rows = tokens[0]

    def columns(which):
        early = jnp.concatenate(
            [
                lax.dynamic_slice_in_dim(in_weight, inner + half * which, half, 1),
                lax.dynamic_slice_in_dim(in_weight, 2 * inner + state_width * which, state_width, 1),
                in_weight[:, 2 * inner + 2 * state_width :],
            ],
            axis=1,
        )
        return early, lax.dynamic_slice_in_dim(in_weight, half * which, half, 1)

    mine, mine_gate = columns(core)
    other, other_gate = columns(1 - core)

    def paired(kept, sent):
        received = swapped(sent)
        return jnp.where(
            core == 0,
            jnp.concatenate([kept, received], axis=0),
            jnp.concatenate([received, kept], axis=0),
        )

    early_weight = lax.all_gather(paired(mine, other), SEQ, axis=0, tiled=True)
    gate_weight = lax.all_gather(paired(mine_gate, other_gate), SEQ, axis=0, tiled=True)
    edge = lax.dynamic_slice_in_dim(own_rows, shard_blocks * BLOCK - EDGE, EDGE, 0)
    own_all = jnp.concatenate([own_rows, passed_along(edge, SEQ, 1)], axis=0)
    other_all = swapped(own_all)

    def projected(rows, weight):
        return jnp.dot(rows, weight, preferred_element_type=F32).astype(BF16)

    got = swapped(projected(other_all, early_weight)[:, : half + state_width])
    kept = projected(own_all, early_weight)
    raw_step = kept[:slots, half + state_width :].astype(F32)
    low = jnp.where(core == 0, kept[:, : half + state_width], got)
    high = jnp.where(core == 0, got, kept[:, : half + state_width])
    mixed = jnp.concatenate([low[:, :half], high[:, :half], low[:, half:], high[:, half:]], axis=1)
    extended = jnp.concatenate([mixed[slots + EDGE - kernel + 1 :], mixed[:slots]], axis=0)
    convolved = jnp.zeros((slots, mixed.shape[1]), F32) + conv_bias[None, :]
    for offset in range(kernel):
        convolved = convolved + conv_weight[offset][None, :] * extended[
            offset : offset + slots
        ].astype(F32)
    conv_out = jax.nn.silu(convolved).astype(BF16)
    live_mask = jnp.arange(slots)[:, None] < shard_blocks * BLOCK
    step_size = jnp.where(live_mask, jax.nn.softplus(raw_step + dt_bias[None, :]), 0.0)
    pieces = []
    log_total = jnp.zeros((heads,), F32)
    summary_state = jnp.zeros((heads, head_dim, state_width), F32)
    for place in range(capacity):
        lower = place * BLOCK
        upper = lower + BLOCK
        in_values = conv_out[lower:upper, :inner].astype(F32).reshape(BLOCK, heads, head_dim)
        in_map = conv_out[lower:upper, inner : inner + state_width]
        out_map = conv_out[lower:upper, inner + state_width :]
        inner_out, cumulative, local_state = block_terms(
            in_values, in_map, out_map, step_size[lower:upper], decay_rate
        )
        block_decay = jnp.exp(cumulative[:, -1])
        summary_state = block_decay[:, None, None] * summary_state + local_state
        log_total = log_total + cumulative[:, -1]
        pieces.append((in_values, out_map, inner_out, cumulative, local_state, block_decay))
    state = incoming_state(log_total, summary_state)
    gate_weight, _ = lax.optimization_barrier((gate_weight, summary_state))

    got_gate = swapped(projected(other_all[:slots], gate_weight))
    kept_gate = projected(own_rows, gate_weight)
    gate = jnp.concatenate(
        [jnp.where(core == 0, kept_gate, got_gate), jnp.where(core == 0, got_gate, kept_gate)],
        axis=1,
    ).astype(F32)
    results = []
    for in_values, out_map, inner_out, cumulative, local_state, block_decay in pieces:
        result = (
            inner_out + carried(out_map, cumulative, state) + skip_gain[None, :, None] * in_values
        )
        results.append(result.reshape(BLOCK, inner))
        state = block_decay[:, None, None] * state + local_state
    scanned = jnp.concatenate(results, axis=0)
    gated = scanned * jax.nn.silu(gate)
    normed = (
        gated
        * lax.rsqrt(jnp.mean(gated * gated, axis=1, keepdims=True) + 1e-05)
        * norm_gain[None, :]
    )
    layer_out = jnp.where(live_mask, normed, 0.0).astype(BF16)
    return layer_out[None]


def solution(mesh):
    split = Mesh(
        mesh.devices.reshape(4, 4, 4, mesh.shape["fsdp"]), ("seq_0", "seq_1", "seq_2", "fsdp")
    )
    return jax.shard_map(
        local,
        mesh=split,
        in_specs=(
            P("fsdp", SEQ, None),
            P("fsdp", SEQ, None),
            P(SEQ_FSDP, None),
            P(),
            P(),
            P(),
            P(),
            P(),
            P(),
        ),
        out_specs=P("fsdp", SEQ, None),
        check_vma=False,
    )
```

time: 460 us -> 282 us (0.61)
  waiting for transfers between devices: 245 us -> 87.2 us
  blocking collectives: 29.7 us -> 0 us
  local copies, waits for them, and re-layouts: 54 us -> 37.5 us
  starting transfers between devices: 3.67 us -> 17.7 us
  other arithmetic: 46.4 us -> 52.6 us
  matrix products: 57 us -> 63.1 us
    all_gather x4 -> x2, waiting for transfers between devices: 244 us -> 57.1 us  [the longest x1 57.1 us: local(): early_weight = lax.all_gather(paired(mine, other), SEQ, axis=0, tiled=True)]
    unnamed x60 -> x74, local copies, waits for them, and re-layouts: 41 us -> 4.53 us
    all_to_all x0 -> x2, waiting for transfers between devices: none -> 20.5 us  [the longest x1 12.5 us: incoming_state(): back = lax.all_to_all(before, SEQ, 0, 0, tiled=True)]
    all_gather x2 -> x0, blocking collectives: 20 us -> none  [prefix_by_axis(): pieces = jax.tree.map(lambda part: lax.all_gather(part, axis), total)]
    concatenate x0 -> x5, other arithmetic: none -> 18.2 us  [the longest x1 11.5 us: local(): jnp.concatenate([low[:, :half], high[:, :half], low[:, half:], high[:, ha...]
    add x3 -> x0, other arithmetic: 16 us -> none  [compose(): later[0][:, None, None] * earlier[1] + later[1]]
    all_to_all x0 -> x2, starting transfers between devices: none -> 13.4 us  [the longest x1 8.61 us: incoming_state(): got = lax.all_to_all(payload, SEQ, 0, 0, tiled=True)]
    unnamed x1 -> x0, blocking collectives: 9.73 us -> none
  transfers between devices with their start and end apart: 5 -> 10, of which waited for: 4 -> 6; matrix products, arithmetic and copies ran while one was open for 3% -> 37% of each run, Pallas kernels for 0% -> 1%
where the time goes in v1:
time: 282 us; the launch traced here: 277 us
  waiting for transfers between devices  87.2 us (31%)
  matrix products  63.1 us (22%)
  other arithmetic  52.6 us (19%)
  local copies, waits for them, and re-layouts  37.5 us (13%)
  starting transfers between devices  17.7 us (6%)
  between operations  15.6 us (6%)
  Pallas kernels  3.1 us (1%)
    all_gather x1, waiting for transfers between devices, local(): early_weight = lax.all_gather(paired(mine, other), SEQ, axis=0, tiled=True)  57.1 us
    dot_general x4, matrix products, projected(): return jnp.dot(rows, weight, preferred_element_type=F32).astype(BF16)  32.9 us
    dot_general x3, matrix products, block_terms(): jnp.einsum('hij,jhp->ihp', mixing, head_input, precision=lax.Precision.HIGH)  15.9 us
    all_to_all x1, waiting for transfers between devices, incoming_state(): back = lax.all_to_all(before, SEQ, 0, 0, tiled=True)  12.5 us
    concatenate x1, other arithmetic, local(): jnp.concatenate([low[:, :half], high[:, :half], low[:, half:], high[:, ha...  11.5 us
    convert_element_type x1, other arithmetic, local(): layer_out = jnp.where(live_mask, normed, 0.0).astype(BF16)  8.79 us
    all_to_all x1, starting transfers between devices, incoming_state(): got = lax.all_to_all(payload, SEQ, 0, 0, tiled=True)  8.61 us
    all_to_all x1, waiting for transfers between devices, incoming_state(): got = lax.all_to_all(payload, SEQ, 0, 0, tiled=True)  8.01 us
  transfers between devices with their start and end apart: 10, of which 6 were waited for; matrix products, arithmetic and copies ran while one was open for 37% of the time, Pallas kernels for 1%

profile of v1, /device:TPU:0, one launch (start us, length us, event | category | flops | bytes accessed | tf_op | source)
XLA Modules:
  0.0 276.9 jit_solution(5313146190333841214)
XLA Ops:
  8.1 1.1 constant_dynamic-slice_fusion.1
  9.3 1.2 collective-permute-done.1
  11.4 1.3 fusion.107
  14.6 3.5 %collective-permute-start = (bf16[8,2560]{1,0:T(8,128)(2,1)S(1)}, bf16[8,2560]{1,0:T(8,128)(2,1)S(1)}, u32[]{:S(2)}, u32[]{:S(2)}) collective-permute-start(bf16[8,2560]{1,0:T(8,128)(2,1)S(1)} %dynamic-slice_bitcast_fusion), channel_id=1, source_target_pairs={{0,2},{2,4},{4,6},{6,8},{8,10},{10,12},{12,14},{14,16},{16,18},{18... | collective-permute-start | bytes 122888 | tf_op jit(solution)/shard_map/ppermute | solution.py:20
  18.1 1.7 collective-permute-done
  19.7 4.3 %pad_maximum_fusion.6 = bf16[776,2560]{1,0:T(8,128)(2,1)} fusion(bf16[8,2560]{1,0:T(8,128)(2,1)S(1)} %collective-permute-done, bf16[768,2560]{1,0:T(8,128)(2,1)} %bitcast.141), kind=kLoop, calls=%fused_computation.62 | loop fusion | flops 7946240 | bytes 7946240 | tf_op jit(solution)/shard_map/concatenate | solution.py:123
  24.6 6.7 %collective-permute-done.4 = bf16[20,1280]{1,0:T(8,128)(2,1)S(1)} collective-permute-done((bf16[20,1280]{1,0:T(8,128)(2,1)S(1)}, bf16[20,1280]{1,0:T(8,128)(2,1)S(1)}, u32[]{:S(2)}, u32[]{:S(2)}) %collective-permute-start.4) | collective-permute-done | bytes 51232 | tf_op jit(solution)/shard_map/ppermute | solution.py:24
  33.3 57.1 %all-gather.3.cloned.1.call-done = bf16[2560,1448]{1,0:T(8,128)(2,1)} async-done(((bf16[40,1448]{1,0:T(8,128)(2,1)}), bf16[2560,1448]{1,0:T(8,128)(2,1)}) %all-gather.3.cloned.1.call-update) | async-done | bytes 7413776 | tf_op jit(solution)/shard_map/all_gather | solution.py:120
  90.4 10.0 %fusion.108 = bf16[776,1448]{1,0:T(8,128)(2,1)S(1)} fusion(bf16[776,2560]{1,0:T(8,128)(2,1)} %collective-permute-done.2, bf16[2560,1448]{1,0:T(8,128)(2,1)} %all-gather.3.cloned.1.call-done), kind=kOutput, calls=%fused_computation.173 | convolution fusion | flops 5753077760 | bytes 13634176 | tf_op jit(solution)/shard_map/dot_general | solution.py:127
  100.4 1.5 slice.284
  102.1 1.2 copy-done.11
  103.3 6.6 %convolution_convert_fusion = bf16[776,1448]{1,0:T(8,128)(2,1)S(1)} fusion(bf16[2560,1448]{1,0:T(8,128)(2,1)S(1)} %copy-done.34, bf16[8,2560]{1,0:T(8,128)(2,1)S(1)} %collective-permute-done, bf16[768,2560]{1,0:T(8,128)(2,1)S(1)} %bitcast.142), kind=kOutput, calls=%fused_computation.65 | convolution fusion | flops 5762147840 | bytes 13634176 | tf_op jit(solution)/shard_map/dot_general | solution.py:127
  120.9 1.6 copy.62
  122.5 1.6 copy.63
  124.8 1.6 copy.59
  127.1 1.6 copy.45
  128.7 2.0 broadcast_select_fusion.1
  130.9 11.5 %pad_maximum_fusion.3 = bf16[768,2816]{1,0:T(8,128)(2,1)S(1)} fusion(bf16[776,128]{1,0:T(8,128)(2,1)S(1)} %slice.177, bf16[776,128]{1,0:T(8,128)(2,1)S(1)} %slice.176, bf16[776,1280]{1,0:T(8,128)(2,1)S(1)} %slice.175, bf16[776,1280]{1,0:T(8,128)(2,1)S(1)} %slice.174), kind=kLoop, calls=%fused_computation.59 | loop fusion | flops 17301504 | bytes 8695808 | tf_op jit(solution)/shard_map/concatenate | solution.py:134
  142.4 1.2 fusion.48
  143.6 6.0 %multiply_convert_fusion = bf16[768,2816]{1,0:T(8,128)(2,1)S(1)} fusion(bf16[768,2816]{1,0:T(8,128)(2,1)S(1)} %pad_maximum_fusion.3, bf16[771,2816]{1,0:T(8,128)(2,1)S(1)} %fusion.48, f32[2816]{0:T(1024)S(1)} %get-tuple-element.9, f32[2816]{0:T(1024)S(1)} %copy-done.14, f32[2816]{0:T(1024)S(1)} %get-tuple-element.8, f32[2816]{0:T(1024)S(1)} %get-tuple-element.7, ...), kind=kLoop, calls=%fused_computation.22 | loop fusion | flops 36765696 | bytes 21683200 | tf_op jit(solution)/shard_map/convert_element_type | solution.py:141
  149.6 2.0 copy-done
  151.6 1.4 fusion.106
  153.0 1.5 copy.54
  155.1 2.1 copy.39
  157.2 1.9 fusion.57
  159.1 1.8 fusion.55
  160.9 1.7 fusion.67
  162.7 1.3 select_maximum_fusion
  164.0 8.6 %all-to-all-start = ((f32[64,48,128]{2,1,0:T(8,128)}), f32[64,48,128]{2,1,0:T(8,128)S(1)}, u32[]{:S(2)}, u32[]{:S(2)}) async-start(f32[64,48,128]{2,1,0:T(8,128)} %select_maximum_fusion), calls=%async_computation | async-start | bytes 3145728 | tf_op jit(solution)/shard_map/all_to_all | solution.py:72
  172.6 9.8 %fusion.51 = bf16[768,1280]{0,1:T(8,128)(2,1)} fusion(bf16[2560,1280]{1,0:T(8,128)(2,1)} %all-gather.5.cloned.1.call-done, bf16[776,2560]{1,0:T(8,128)(2,1)} %collective-permute-done.2), kind=kOutput, calls=%fused_computation.66 | convolution fusion | flops 5034147840 | bytes 12451840 | tf_op jit(solution)/shard_map/dot_general | solution.py:127
  182.4 6.5 %fusion.54 = bf16[768,1280]{0,1:T(8,128)(2,1)} fusion(bf16[2560,1280]{1,0:T(8,128)(2,1)S(1)} %copy-done.35, bf16[1,768,2560]{2,1,0:T(8,128)(2,1)S(1)} %copy-done.12), kind=kOutput, calls=%fused_computation.74 | convolution fusion | flops 5034147840 | bytes 12451840 | tf_op jit(solution)/shard_map/dot_general | solution.py:127
  189.0 8.0 %all-to-all-done.got_ref = f32[64,48,128]{2,1,0:T(8,128)S(1)} async-done(((f32[64,48,128]{2,1,0:T(8,128)}), f32[64,48,128]{2,1,0:T(8,128)S(1)}, u32[]{:S(2)}, u32[]{:S(2)}) %all-to-all-start) | async-done | bytes 1572896 | tf_op jit(solution)/shard_map/all_to_all | solution.py:72
  197.0 1.2 copy-done.4
  198.1 3.1 %prefix.1 = f32[64,40,128]{2,1,0:T(8,128)} custom-call(f32[64,48,128]{2,1,0:T(8,128)} %copy-done.4), custom_call_target="tpu_custom_call" | custom-call | flops 8000000 | bytes 1500000 | tf_op jit(solution)/shard_map/prefix/pallas_call | solution.py:73
  201.2 4.8 %all-to-all-start.1 = ((f32[64,40,128]{2,1,0:T(8,128)}), f32[64,40,128]{2,1,0:T(8,128)S(1)}, u32[]{:S(2)}, u32[]{:S(2)}) async-start(f32[64,40,128]{2,1,0:T(8,128)} %prefix.1), calls=%async_computation.1 | async-start | bytes 2621440 | tf_op jit(solution)/shard_map/all_to_all | solution.py:79
  206.1 1.1 fusion.85
  207.1 1.1 fusion.88
  209.3 4.4 %broadcast_select_fusion.3 = (bf16[768,1280]{0,1:T(8,128)(2,1)}, bf16[768,1280]{0,1:T(8,128)(2,1)}) fusion(bf16[768,1280]{0,1:T(8,128)(2,1)} %fusion.54, bf16[768,1280]{0,1:T(8,128)(2,1)} %collective-permute-done.5, pred[]{:T(512)S(6)} %eq.2), kind=kLoop, calls=%fused_computation.87 | loop fusion | flops 1966080 | bytes 7864321 | tf_op jit(solution)/shard_map/jit(_where)/select_n | solution.py:166
  213.6 12.5 %all-to-all-done.1 = f32[64,40,128]{2,1,0:T(8,128)S(1)} async-done(((f32[64,40,128]{2,1,0:T(8,128)}), f32[64,40,128]{2,1,0:T(8,128)S(1)}, u32[]{:S(2)}, u32[]{:S(2)}) %all-to-all-start.1) | async-done | bytes 1310752 | tf_op jit(solution)/shard_map/all_to_all | solution.py:79
  226.1 2.2 fusion.68
  228.4 1.8 fusion.76
  230.3 1.7 fusion.82
  232.1 5.2 %fusion.60 = f32[256,40,64]{0,2,1:T(8,128)S(1)} fusion(bf16[256,40,64]{0,2,1:T(8,128)(2,1)S(1)} %bitcast.139, f32[256,40,64]{0,2,1:T(8,128)S(1)} %fusion.68, f32[40,256]{1,0:T(8,128)S(1)} %copy-done.23, f32[40,256]{1,0:T(8,128)S(1)} %copy-done.18, f32[256,256]{1,0:T(8,128)S(1)} %fusion.85, pred[256,256]{1,0:T(8,128)(4,1)S(1)} %copy-done.13, ...), kind=kOutput, calls=%fused_computation.80 | convolution fusion | flops 1020395520 | bytes 7004320 | tf_op jit(solution)/shard_map/hij,jhp->ihp/dot_general | solution.py:36
  237.4 5.5 %fusion.58 = f32[256,40,64]{0,2,1:T(8,128)S(1)} fusion(bf16[256,40,64]{0,2,1:T(8,128)(2,1)S(1)} %bitcast.137, f32[256,40,64]{0,2,1:T(8,128)S(1)} %fusion.76, f32[40,256]{1,0:T(8,128)S(1)} %copy-done.21, f32[40,256]{1,0:T(8,128)S(1)} %copy-done.17, f32[256,256]{1,0:T(8,128)S(1)} %fusion.88, pred[256,256]{1,0:T(8,128)(4,1)S(1)} %copy-done.13, ...), kind=kOutput, calls=%fused_computation.78 | convolution fusion | flops 1020395520 | bytes 7004320 | tf_op jit(solution)/shard_map/hij,jhp->ihp/dot_general | solution.py:36
  242.9 5.2 %fusion.56 = f32[256,40,64]{0,2,1:T(8,128)S(1)} fusion(bf16[256,40,64]{0,2,1:T(8,128)(2,1)S(1)} %bitcast.135, f32[256,40,64]{0,2,1:T(8,128)S(1)} %fusion.82, f32[40,256]{1,0:T(8,128)S(1)} %copy-done.19, f32[40,256]{1,0:T(8,128)S(1)} %copy-done.16, f32[256,256]{1,0:T(8,128)S(1)} %fusion.95, pred[256,256]{1,0:T(8,128)(4,1)S(1)} %copy-done.13, ...), kind=kOutput, calls=%fused_computation.76 | convolution fusion | flops 1020395520 | bytes 7004320 | tf_op jit(solution)/shard_map/hij,jhp->ihp/dot_general | solution.py:36
  248.1 6.6 %fusion.29 = f32[768]{0:T(1024)S(1)} fusion(f32[256,2560]{0,1:T(8,128)S(1)} %bitcast.128, f32[256,2560]{0,1:T(8,128)S(1)} %bitcast.130, f32[256,2560]{0,1:T(8,128)S(1)} %bitcast.132, bf16[768,1280]{0,1:T(8,128)(2,1)S(1)} %copy-done.2, bf16[768,1280]{0,1:T(8,128)(2,1)S(1)} %copy-done.1), kind=kLoop, calls=%fused_computation.35 | loop fusion | flops 25558272 | bytes 11799552 | tf_op jit(solution)/shard_map/reduce_sum | solution.py:180
  254.7 8.8 %select_convert_fusion = bf16[1,768,2560]{1,2,0:T(8,128)(2,1)} fusion(f32[1,256,2560]{1,2,0:T(8,128)S(1)} %bitcast.129, f32[1,256,2560]{1,2,0:T(8,128)S(1)} %bitcast.131, f32[1,256,2560]{1,2,0:T(8,128)S(1)} %bitcast.133, bf16[1,768,1280]{1,2,0:T(8,128)(2,1)S(1)} %bitcast.127, bf16[1,768,1280]{1,2,0:T(8,128)(2,1)S(1)} %bitcast.126, f32[2560]{0:T(1024)S(1)} %copy-done.26, ...), kind=kLoop, calls=%fused_computation.34 | loop fusion | flops 29491200 | bytes 15742720 | tf_op jit(solution)/shard_map/convert_element_type | solution.py:183
  263.5 6.3 %copy.65 = bf16[1,768,2560]{2,1,0:T(8,128)(2,1)} copy(bf16[1,768,2560]{1,2,0:T(8,128)(2,1)} %select_convert_fusion) | data formatting | bytes 7864320 | tf_op jit(solution)/shard_map/convert_element_type | solution.py:183
  (137 shorter events, 20.3 us)
Async XLA Ops:
  6.5 83.9 %all-gather.3.cloned.1.call-start = ((), (), s32[]{:S(2)}) async-start(), calls=%async_computation.2 | async-start | bytes 7987200 | tf_op jit(solution)/shard_map/all_gather | solution.py:120
  9.2 1.3 collective-permute-start.1
  11.3 161.3 %all-gather.5.cloned.1.call-start = ((), (), s32[]{:S(2)}) async-start(), calls=%async_computation.3 | async-start | bytes 6656000 | tf_op jit(solution)/shard_map/all_gather | solution.py:121
  14.6 5.2 %collective-permute-start = (bf16[8,2560]{1,0:T(8,128)(2,1)S(1)}, bf16[8,2560]{1,0:T(8,128)(2,1)S(1)}, u32[]{:S(2)}, u32[]{:S(2)}) collective-permute-start(bf16[8,2560]{1,0:T(8,128)(2,1)S(1)} %dynamic-slice_bitcast_fusion), channel_id=1, source_target_pairs={{0,2},{2,4},{4,6},{6,8},{8,10},{10,12},{12,14},{14,16},{16,18},{18... | collective-permute-start | bytes 122888 | tf_op jit(solution)/shard_map/ppermute | solution.py:20
  19.7 12.9 %copy-start.15 = (f32[4,2816]{1,0:T(4,128)S(1)}, f32[4,2816]{1,0:T(4,128)}, u32[]{:S(2)}) copy-start(f32[4,2816]{1,0:T(4,128)} %param.12) | copy-start | bytes 135172
  24.0 9.3 %collective-permute-start.2 = (bf16[776,2560]{1,0:T(8,128)(2,1)}, bf16[776,2560]{1,0:T(8,128)(2,1)}, u32[]{:S(2)}, u32[]{:S(2)}) collective-permute-start(bf16[776,2560]{1,0:T(8,128)(2,1)} %pad_maximum_fusion.6), channel_id=1, source_target_pairs={{0,1},{1,0},{2,3},{3,2},{4,5},{5,4},{6,7},{7,6},{8,9},{9,8},{10,11... | collective-permute-start | bytes 11919368 | tf_op jit(solution)/shard_map/ppermute | solution.py:24
  24.0 7.2 %collective-permute-start.4 = (bf16[20,1280]{1,0:T(8,128)(2,1)S(1)}, bf16[20,1280]{1,0:T(8,128)(2,1)S(1)}, u32[]{:S(2)}, u32[]{:S(2)}) collective-permute-start(bf16[20,1280]{1,0:T(8,128)(2,1)S(1)} %get-tuple-element.33), channel_id=1, source_target_pairs={{0,1},{1,0},{2,3},{3,2},{4,5},{5,4},{6,7},{7,6},{8,9},{9,8},{10,11... | collective-permute-start | bytes 153608 | tf_op jit(solution)/shard_map/ppermute | solution.py:24
  32.0 78.0 %copy-start.28 = (pred[768]{0:T(1024)(128)(4,1)}, pred[768]{0:T(1024)(128)(4,1)S(1)}, u32[]{:S(2)}) copy-start(pred[768]{0:T(1024)(128)(4,1)S(1)} %iota_compare_fusion.2) | copy-start | bytes 2308
  90.4 11.7 %copy-start.34 = (bf16[2560,1448]{1,0:T(8,128)(2,1)S(1)}, bf16[2560,1448]{1,0:T(8,128)(2,1)}, u32[]{:S(2)}) copy-start(bf16[2560,1448]{1,0:T(8,128)(2,1)} %all-gather.3.cloned.1.call-done) | copy-start | bytes 22241284
  100.4 2.9 %copy-start.11 = (bf16[1,768,2560]{2,1,0:T(8,128)(2,1)S(1)}, bf16[1,768,2560]{2,1,0:T(8,128)(2,1)}, u32[]{:S(2)}) copy-start(bf16[1,768,2560]{2,1,0:T(8,128)(2,1)} %param.9) | copy-start | bytes 11796484
  101.9 8.1 %copy-start.33 = (f32[40]{0:T(128)S(1)}, f32[40]{0:T(128)}, u32[]{:S(2)}) copy-start(f32[40]{0:T(128)} %param.14) | copy-start | bytes 484
  101.9 8.3 %copy-start.32 = (f32[40]{0:T(128)S(1)}, f32[40]{0:T(128)}, u32[]{:S(2)}) copy-start(f32[40]{0:T(128)} %param.15) | copy-start | bytes 484
  101.9 26.7 %collective-permute-start.3 = (bf16[776,1408]{1,0:T(8,128)(2,1)}, bf16[776,1408]{1,0:T(8,128)(2,1)}, u32[]{:S(2)}, u32[]{:S(2)}) collective-permute-start(bf16[776,1408]{1,0:T(8,128)(2,1)} %slice.284), channel_id=1, source_target_pairs={{0,1},{1,0},{2,3},{3,2},{4,5},{5,4},{6,7},{7,6},{8,9},{9,8},{10,11... | collective-permute-start | bytes 6555656 | tf_op jit(solution)/shard_map/ppermute | solution.py:24
  142.4 1.2 copy-start.14
  142.4 1.2 copy-start.25
  149.6 2.0 copy-start
  155.1 4.0 %copy-start.7 = (bf16[256,2560]{0,1:T(8,128)(2,1)}, bf16[256,2560]{0,1:T(8,128)(2,1)S(1)}, u32[]{:S(2)}) copy-start(bf16[256,2560]{0,1:T(8,128)(2,1)S(1)} %copy.52) | copy-start | bytes 3932164
  155.1 5.8 %copy-start.27 = (f32[40]{0:T(128)S(1)}, f32[40]{0:T(128)}, u32[]{:S(2)}) copy-start(f32[40]{0:T(128)} %get-tuple-element.42) | copy-start | bytes 484
  155.1 5.8 %copy-start.30 = (f32[40]{0:T(128)S(1)}, f32[40]{0:T(128)}, u32[]{:S(2)}) copy-start(f32[40]{0:T(128)} %get-tuple-element.41) | copy-start | bytes 484
  155.1 5.8 %copy-start.31 = (f32[40]{0:T(128)S(1)}, f32[40]{0:T(128)}, u32[]{:S(2)}) copy-start(f32[40]{0:T(128)} %get-tuple-element.43) | copy-start | bytes 484
  157.2 5.5 %copy-start.5 = (bf16[256,2560]{0,1:T(8,128)(2,1)}, bf16[256,2560]{0,1:T(8,128)(2,1)S(1)}, u32[]{:S(2)}) copy-start(bf16[256,2560]{0,1:T(8,128)(2,1)S(1)} %copy.39) | copy-start | bytes 3932164
  157.2 3.7 %copy-start.9 = (bf16[256,2560]{0,1:T(8,128)(2,1)S(1)}, bf16[256,2560]{0,1:T(8,128)(2,1)}, u32[]{:S(2)}) copy-start(bf16[256,2560]{0,1:T(8,128)(2,1)} %copy.54) | copy-start | bytes 3932164
  159.1 3.6 %copy-start.3 = (f32[40,64,128]{2,1,0:T(8,128)}, f32[40,64,128]{2,1,0:T(8,128)S(1)}, u32[]{:S(2)}) copy-start(f32[40,64,128]{2,1,0:T(8,128)S(1)} %fusion.57) | copy-start | bytes 3932164
  164.0 33.0 %all-to-all-start = ((f32[64,48,128]{2,1,0:T(8,128)}), f32[64,48,128]{2,1,0:T(8,128)S(1)}, u32[]{:S(2)}, u32[]{:S(2)}) async-start(f32[64,48,128]{2,1,0:T(8,128)} %select_maximum_fusion), calls=%async_computation | async-start | bytes 3145728 | tf_op jit(solution)/shard_map/all_to_all | solution.py:72
  172.6 9.8 %copy-start.12 = (bf16[1,768,2560]{2,1,0:T(8,128)(2,1)S(1)}, bf16[1,768,2560]{2,1,0:T(8,128)(2,1)}, u32[]{:S(2)}) copy-start(bf16[1,768,2560]{2,1,0:T(8,128)(2,1)} %param.9) | copy-start | bytes 11796484
  172.6 9.8 %copy-start.35 = (bf16[2560,1280]{1,0:T(8,128)(2,1)S(1)}, bf16[2560,1280]{1,0:T(8,128)(2,1)}, u32[]{:S(2)}) copy-start(bf16[2560,1280]{1,0:T(8,128)(2,1)} %all-gather.5.cloned.1.call-done) | copy-start | bytes 19660804
  182.4 26.8 %collective-permute-start.5 = (bf16[768,1280]{0,1:T(8,128)(2,1)}, bf16[768,1280]{0,1:T(8,128)(2,1)}, u32[]{:S(2)}, u32[]{:S(2)}) collective-permute-start(bf16[768,1280]{0,1:T(8,128)(2,1)} %fusion.51), channel_id=1, source_target_pairs={{0,1},{1,0},{2,3},{3,2},{4,5},{5,4},{6,7},{7,6},{8,9},{9,8},{10,11... | collective-permute-start | bytes 5898248 | tf_op jit(solution)/shard_map/ppermute | solution.py:24
  197.0 1.2 copy-start.4
  201.2 24.9 %all-to-all-start.1 = ((f32[64,40,128]{2,1,0:T(8,128)}), f32[64,40,128]{2,1,0:T(8,128)S(1)}, u32[]{:S(2)}, u32[]{:S(2)}) async-start(f32[64,40,128]{2,1,0:T(8,128)} %prefix.1), calls=%async_computation.1 | async-start | bytes 2621440 | tf_op jit(solution)/shard_map/all_to_all | solution.py:79
  228.4 3.6 %copy-start.10 = (bf16[256,2560]{0,1:T(8,128)(2,1)S(1)}, bf16[256,2560]{0,1:T(8,128)(2,1)}, u32[]{:S(2)}) copy-start(bf16[256,2560]{0,1:T(8,128)(2,1)} %copy.54) | copy-start | bytes 3932164
  228.4 3.6 %copy-start.13 = (pred[256,256]{1,0:T(8,128)(4,1)S(1)}, pred[256,256]{1,0:T(8,128)(4,1)}, u32[]{:S(2)}) copy-start(pred[256,256]{1,0:T(8,128)(4,1)} %iota_compare_fusion.1) | copy-start | bytes 196612
  228.4 3.6 %copy-start.18 = (f32[40,256]{1,0:T(8,128)S(1)}, f32[40,256]{1,0:T(8,128)}, u32[]{:S(2)}) copy-start(f32[40,256]{1,0:T(8,128)} %copy.60) | copy-start | bytes 122884
  228.4 3.6 %copy-start.23 = (f32[40,256]{1,0:T(8,128)S(1)}, f32[40,256]{1,0:T(8,128)}, u32[]{:S(2)}) copy-start(f32[40,256]{1,0:T(8,128)} %copy.62) | copy-start | bytes 122884
  228.4 3.6 %copy-start.24 = (f32[256,40]{0,1:T(8,128)S(1)}, f32[256,40]{0,1:T(8,128)}, u32[]{:S(2)}) copy-start(f32[256,40]{0,1:T(8,128)} %copy.63) | copy-start | bytes 122884
  228.4 3.6 %copy-start.36 = (f32[40]{0:T(128)S(1)}, f32[40]{0:T(128)}, u32[]{:S(2)}) copy-start(f32[40]{0:T(128)} %param.16) | copy-start | bytes 484
  232.0 5.3 %copy-start.8 = (bf16[256,2560]{0,1:T(8,128)(2,1)S(1)}, bf16[256,2560]{0,1:T(8,128)(2,1)}, u32[]{:S(2)}) copy-start(bf16[256,2560]{0,1:T(8,128)(2,1)} %copy-done.7) | copy-start | bytes 3932164
  232.0 5.3 %copy-start.17 = (f32[40,256]{1,0:T(8,128)S(1)}, f32[40,256]{1,0:T(8,128)}, u32[]{:S(2)}) copy-start(f32[40,256]{1,0:T(8,128)} %copy.56) | copy-start | bytes 122884
  232.0 5.3 %copy-start.21 = (f32[40,256]{1,0:T(8,128)S(1)}, f32[40,256]{1,0:T(8,128)}, u32[]{:S(2)}) copy-start(f32[40,256]{1,0:T(8,128)} %copy.58) | copy-start | bytes 122884
  232.0 5.3 %copy-start.22 = (f32[256,40]{0,1:T(8,128)S(1)}, f32[256,40]{0,1:T(8,128)}, u32[]{:S(2)}) copy-start(f32[256,40]{0,1:T(8,128)} %copy.59) | copy-start | bytes 122884
  237.3 5.5 %copy-start.6 = (bf16[256,2560]{0,1:T(8,128)(2,1)S(1)}, bf16[256,2560]{0,1:T(8,128)(2,1)}, u32[]{:S(2)}) copy-start(bf16[256,2560]{0,1:T(8,128)(2,1)} %copy-done.5) | copy-start | bytes 3932164
  237.3 5.5 %copy-start.16 = (f32[40,256]{1,0:T(8,128)S(1)}, f32[40,256]{1,0:T(8,128)}, u32[]{:S(2)}) copy-start(f32[40,256]{1,0:T(8,128)} %copy.42) | copy-start | bytes 122884
  237.3 5.5 %copy-start.19 = (f32[40,256]{1,0:T(8,128)S(1)}, f32[40,256]{1,0:T(8,128)}, u32[]{:S(2)}) copy-start(f32[40,256]{1,0:T(8,128)} %copy.44) | copy-start | bytes 122884
  237.3 5.5 %copy-start.20 = (f32[256,40]{0,1:T(8,128)S(1)}, f32[256,40]{0,1:T(8,128)}, u32[]{:S(2)}) copy-start(f32[256,40]{0,1:T(8,128)} %copy.45) | copy-start | bytes 122884
  242.8 5.3 %copy-start.1 = (bf16[768,1280]{0,1:T(8,128)(2,1)S(1)}, bf16[768,1280]{0,1:T(8,128)(2,1)}, u32[]{:S(2)}) copy-start(bf16[768,1280]{0,1:T(8,128)(2,1)} %get-tuple-element.16) | copy-start | bytes 5898244
  242.9 5.2 %copy-start.2 = (bf16[768,1280]{0,1:T(8,128)(2,1)S(1)}, bf16[768,1280]{0,1:T(8,128)(2,1)}, u32[]{:S(2)}) copy-start(bf16[768,1280]{0,1:T(8,128)(2,1)} %get-tuple-element.17) | copy-start | bytes 5898244
  248.1 6.6 %copy-start.26 = (f32[2560]{0:T(1024)S(1)}, f32[2560]{0:T(1024)}, u32[]{:S(2)}) copy-start(f32[2560]{0:T(1024)} %param.17) | copy-start | bytes 30724
  248.1 6.6 %copy-start.29 = (pred[768]{0:T(1024)(128)(4,1)S(1)}, pred[768]{0:T(1024)(128)(4,1)}, u32[]{:S(2)}) copy-start(pred[768]{0:T(1024)(128)(4,1)} %copy-done.28) | copy-start | bytes 2308
Sparse Core Ops, SparseCore 0:
  11.4 78.9 all-gather.2
  93.3 72.3 all-gather.4

commit v2 on v1

v2 whole, which is shorter than its diff:
```python
import functools

import jax
import jax.numpy as jnp
from jax import lax
from jax.experimental import pallas as pl
from jax.experimental.pallas import tpu as pltpu
from jax.sharding import Mesh
from jax.sharding import PartitionSpec as P

BLOCK = 256
EDGE = 8
SEQ_FSDP = ("seq_0", "seq_1", "seq_2", "fsdp")
SEQ = ("seq_0", "seq_1", "seq_2")
F32 = jnp.float32
BF16 = jnp.bfloat16


def passed_along(value, axis, steps):
    count = lax.axis_size(axis)
    leading, last = (max(0, -steps), min(count, count - steps))
    return lax.ppermute(value, axis, [(source, source + steps) for source in range(leading, last)])


def swapped(value):
    return lax.ppermute(value, "fsdp", [(0, 1), (1, 0)])


def split_dot(left, right, dims):
    high = right.astype(BF16)
    low = (right - high.astype(F32)).astype(BF16)
    dot = lambda part: lax.dot_general(left, part, (dims, ((), ())), preferred_element_type=F32)
    return dot(high) + dot(low)


def spread(table, lanes):
    index = jnp.broadcast_to(lanes, table.shape)
    return jnp.take_along_axis(table, index, axis=1)


def lane_ids(shape):
    return lax.broadcasted_iota(jnp.int32, shape, 1)


def front_kernel(
    heads, head_dim, chunk_rows,
    scalars, kept_ref, got_ref, kept_map_ref, got_map_ref, raw_ref, conv_ref, map_conv_ref, head_ref,
    x_ref, maps_ref, cum_ref, step_ref, pay_ref,
    ext, factor, turned, high, low,
):
    group = pl.program_id(0)
    groups = pl.num_programs(0)
    slots, width = x_ref.shape
    chunk = 128

    def fill(ref):
        ext[:EDGE, :] = ref[slots:, :].astype(F32)
        ext[EDGE:, :] = ref[:slots, :].astype(F32)

    def convolve(taps, start):
        first = EDGE - 3 + start
        total = taps[4:5, :] + taps[0:1, :] * ext[first : first + chunk, :]
        for offset in range(1, 4):
            total = total + taps[offset : offset + 1, :] * ext[first + offset : first + offset + chunk, :]
        return (total * jax.nn.sigmoid(total)).astype(BF16)

    @pl.when(group == 0)
    def _():
        core, live = scalars[0], scalars[1]
        for which in range(2):
            taps = map_conv_ref[:, which * width : (which + 1) * width]

            @pl.when(core == which)
            def _():
                fill(kept_map_ref)

            @pl.when(core != which)
            def _():
                fill(got_map_ref)

            for start in range(0, slots, chunk):
                value = convolve(taps, start)
                maps_ref[start : start + chunk, which * width : (which + 1) * width] = value
                if which == 0:
                    turned[:, start : start + chunk] = value.astype(F32).T.astype(BF16)
        lanes = lane_ids((slots, width))
        rows = lax.broadcasted_iota(jnp.int32, (slots, width), 0)
        shifted = raw_ref[:slots, :].astype(F32) + head_ref[0:1, :]
        step = jnp.maximum(shifted, 0.0) + jnp.log1p(jnp.exp(-jnp.abs(shifted)))
        step = jnp.where((lanes < heads) & (rows < live), step, 0.0)
        step_ref[...] = step
        log_decay = -(step * head_ref[1:2, :])
        triangle = (
            lax.broadcasted_iota(jnp.int32, (BLOCK, BLOCK), 0) >= lane_ids((BLOCK, BLOCK))
        ).astype(F32)
        before = jnp.zeros((1, width), F32)
        for lower in range(0, slots, BLOCK):
            cum = jnp.dot(
                triangle,
                log_decay[lower : lower + BLOCK],
                precision=lax.Precision.HIGHEST,
                preferred_element_type=F32,
            )
            cum_ref[lower : lower + BLOCK, :] = cum
            factor[lower : lower + BLOCK, :] = cum + before
            before = before + cum[BLOCK - 1 :, :]
        factor[...] = jnp.exp(before - factor[...]) * step
        pay_ref[:, chunk_rows:, :] = jnp.broadcast_to(
            before[None], (pay_ref.shape[0], pay_ref.shape[1] - chunk_rows, width)
        )

    @pl.when(group < groups // 2)
    def _():
        fill(kept_ref)

    @pl.when(group >= groups // 2)
    def _():
        fill(got_ref)

    lanes = group * (width // head_dim) + lane_ids((1, width)) // head_dim
    taps = conv_ref[...]
    for start in range(0, slots, chunk):
        value = convolve(taps, start)
        x_ref[start : start + chunk, :] = value
        weighted = value.astype(F32) * spread(factor[start : start + chunk, :], lanes)
        top = weighted.astype(BF16)
        high[start : start + chunk, :] = top
        low[start : start + chunk, :] = (weighted - top.astype(F32)).astype(BF16)
    state = jnp.dot(turned[...], high[...], preferred_element_type=F32) + jnp.dot(
        turned[...], low[...], preferred_element_type=F32
    )
    state = state.T
    pieces = chunk_rows // 8
    for k in range(width // 8):
        place = group * (width // 8) + k
        row = pl.multiple_of(lax.rem(place, pieces) * 8, 8)
        pay_ref[lax.div(place, pieces), pl.ds(row, 8), :] = state[8 * k : 8 * k + 8, :]


def inner_kernel(
    head_dim,
    x_ref, maps_ref, cum_ref, step_ref, skip_ref, y_ref,
    run, scores, turned, across,
):
    block, group = pl.program_id(0), pl.program_id(1)
    rows, width = x_ref.shape
    part = rows // 2

    @pl.when(group == 0)
    def _():
        b = maps_ref[:, :width]
        c = maps_ref[:, width:]
        scores[...] = lax.dot_general(c, b, (((1,), (1,)), ((), ())), preferred_element_type=F32)
        turned[...] = b.astype(F32).T.astype(BF16)
        across[...] = (cum_ref[...] - jnp.log(step_ref[...])).T

    @pl.when(block == 0)
    def _():
        run[group] = jnp.zeros(run.shape[1:], F32)

    first_head = group * (width // head_dim)
    lane = lane_ids((1, width))
    cum = cum_ref[...]
    by_head = [spread(cum, jnp.zeros((1, width), jnp.int32) + first_head + e) for e in range(2)]
    low_lanes = lane_ids((rows, width)) < head_dim
    cum_x = jnp.where(low_lanes, by_head[0], by_head[1])
    step_x = spread(step_ref[...], first_head + lane // head_dim)
    x = x_ref[...]
    causal = lax.broadcasted_iota(jnp.int32, (part, part), 0) >= lane_ids((part, part))
    outs = []
    for e in range(2):
        row = across[pl.ds(first_head + e, 1), :]
        column = by_head[e]

        def mixing(i, j):
            exponent = column[i * part : (i + 1) * part, :] - row[:, j * part : (j + 1) * part]
            if i == j:
                exponent = jnp.where(causal, exponent, -jnp.inf)
            value = jnp.exp(exponent) * scores[i * part : (i + 1) * part, j * part : (j + 1) * part]
            top = value.astype(BF16)
            return top, (value - top.astype(F32)).astype(BF16)

        m00, m10, m11 = mixing(0, 0), mixing(1, 0), mixing(1, 1)
        dot = lambda m, j: jnp.dot(m, x[j * part : (j + 1) * part], preferred_element_type=F32)
        outs.append(
            jnp.concatenate(
                [
                    dot(m00[0], 0) + dot(m00[1], 0),
                    (dot(m10[0], 0) + dot(m10[1], 0)) + (dot(m11[0], 1) + dot(m11[1], 1)),
                ],
                axis=0,
            )
        )
    x32 = x.astype(F32)
    state = run[group]
    reach = split_dot(maps_ref[:, width:], state, ((1,), (0,)))
    y_ref[...] = (
        jnp.where(low_lanes, outs[0], outs[1]) + jnp.exp(cum_x) * reach + skip_ref[0:1, :] * x32
    )
    end = cum_x[rows - 1 :, :]
    weighted = x32 * (jnp.exp(end - cum_x) * step_x)
    run[group] = jnp.exp(end) * state + split_dot(turned[...], weighted, ((1,), (0,)))


def finish_kernel(
    head_dim,
    scalars, kept_ref, got_ref, y_ref, c_ref, cum_ref, state_ref, gain_ref, out_ref,
    high, low, before, gated,
):
    block = pl.program_id(0)
    rows, inner = y_ref.shape
    width = c_ref.shape[1]
    groups = inner // width

    @pl.when(block == 0)
    def _():
        state = state_ref[...]
        top = state.astype(BF16)
        high[...] = top
        low[...] = (state - top.astype(F32)).astype(BF16)
        before[...] = jnp.zeros(before.shape, F32)

    cum = cum_ref[...] + before[0:1, :]
    before[...] = jnp.broadcast_to(cum[rows - 1 :, :], before.shape)
    reached = jnp.exp(cum)
    c = c_ref[...]
    lane = lane_ids((1, width))

    def half(gate_ref, first):
        def body(k, total):
            group = first + k
            at = pl.ds(pl.multiple_of(group * width, width), width)
            dot = lambda part: lax.dot_general(
                c, part[at, :], (((1,), (1,)), ((), ())), preferred_element_type=F32
            )
            carried = spread(reached, group * (width // head_dim) + lane // head_dim) * (
                dot(high) + dot(low)
            )
            gate = gate_ref[:, pl.ds(pl.multiple_of(k * width, width), width)].astype(F32)
            value = (y_ref[:, at] + carried) * (gate * jax.nn.sigmoid(gate))
            gated[:, at] = value
            return total + value * value

        return body

    total = jnp.zeros((rows, width), F32)
    total = lax.fori_loop(0, groups // 2, half(kept_ref, 0), total)
    total = lax.fori_loop(0, groups // 2, half(got_ref, groups // 2), total)
    scale = lax.rsqrt(jnp.sum(total, axis=1, keepdims=True) / inner + 1e-05)
    live = lax.broadcasted_iota(jnp.int32, (rows, 1), 0) + block * rows < scalars[1]
    shift = scalars[0] * (groups // 2)

    def write(group, _):
        at = pl.ds(pl.multiple_of(group * width, width), width)
        target = lax.rem(group + shift, groups)
        value = gated[:, at] * scale * gain_ref[0:1, at]
        out_ref[:, pl.ds(pl.multiple_of(target * width, width), width)] = jnp.where(
            live, value, 0.0
        ).astype(BF16)
        return _

    lax.fori_loop(0, groups, write, 0)


def prefix_kernel(count, rows, head_dim, place_ref, got_ref, out_ref, turned):
    first = lax.div(place_ref[0] * rows, head_dim)
    edge = (first + 1) * head_dim - place_ref[0] * rows
    turned[...] = got_ref[:, rows, :].T
    shape = (rows, count)
    decays = jnp.exp(
        jnp.where(
            lax.broadcasted_iota(jnp.int32, shape, 0) < edge,
            jnp.broadcast_to(turned[pl.ds(first, 1), :], shape),
            jnp.broadcast_to(turned[pl.ds(first + 1, 1), :], shape),
        )
    )
    state = jnp.zeros((rows, got_ref.shape[2]), F32)
    for source in range(count):
        out_ref[source] = state
        if source < count - 1:
            factor = jnp.broadcast_to(decays[:, source : source + 1], state.shape)
            state = state * factor + got_ref[source, :rows, :]


def local(
    tokens, bounds, in_weight, conv_weight, conv_bias, dt_bias, decay_rate, skip_gain, norm_gain
):
    slots = tokens.shape[1]
    inner = norm_gain.shape[0]
    state_width = (conv_bias.shape[0] - inner) // 2
    heads = decay_rate.shape[0]
    head_dim = inner // heads
    kernel = conv_weight.shape[0]
    capacity = slots // BLOCK
    half = inner // 2
    core = lax.axis_index("fsdp")
    shard_blocks = bounds[0, 0, 1] - bounds[0, 0, 0]
    own_rows = tokens[0]

    def turned_by_core(value, which, axis):
        middle = value.shape[axis] // 2
        first = lax.slice_in_dim(value, 0, middle, axis=axis)
        second = lax.slice_in_dim(value, middle, 2 * middle, axis=axis)
        return jnp.where(
            which == 0,
            jnp.concatenate([first, second], axis),
            jnp.concatenate([second, first], axis),
        )

    def columns(which):
        early = jnp.concatenate(
            [
                lax.dynamic_slice_in_dim(in_weight, inner + half * which, half, 1),
                lax.dynamic_slice_in_dim(in_weight, 2 * inner + state_width * which, state_width, 1),
                turned_by_core(in_weight[:, 2 * inner + 2 * state_width :], which, 1),
            ],
            axis=1,
        )
        return early, lax.dynamic_slice_in_dim(in_weight, half * which, half, 1)

    mine, mine_gate = columns(core)
    other, other_gate = columns(1 - core)

    def paired(kept, sent):
        received = swapped(sent)
        return jnp.where(
            core == 0,
            jnp.concatenate([kept, received], axis=0),
            jnp.concatenate([received, kept], axis=0),
        )

    early_weight = lax.all_gather(paired(mine, other), SEQ, axis=0, tiled=True)
    gate_weight = lax.all_gather(paired(mine_gate, other_gate), SEQ, axis=0, tiled=True)
    edge = lax.dynamic_slice_in_dim(own_rows, shard_blocks * BLOCK - EDGE, EDGE, 0)
    own_all = jnp.concatenate([own_rows, passed_along(edge, SEQ, 1)], axis=0)
    other_all = swapped(own_all)

    def projected(rows, weight):
        return jnp.dot(rows, weight, preferred_element_type=F32).astype(BF16)

    groups = inner // state_width
    taps = jnp.pad(
        jnp.concatenate([conv_weight, conv_bias[None, :]], axis=0), ((0, 8 - kernel - 1), (0, 0))
    )
    map_taps = taps[:, inner:]
    taps = turned_by_core(taps[:, :inner], core, 1)
    head_rows = turned_by_core(jnp.stack([dt_bias, decay_rate]), core, 1)
    head_rows = jnp.pad(head_rows, ((0, 6), (0, state_width - heads)))
    skip = jnp.broadcast_to(
        jnp.repeat(turned_by_core(skip_gain, core, 0), head_dim)[None, :], (8, inner)
    )
    gain = jnp.broadcast_to(turned_by_core(norm_gain, core, 0)[None, :], (8, inner))
    scalars = jnp.stack([core.astype(jnp.int32), shard_blocks * BLOCK])
    count = lax.axis_size(SEQ)
    chunk_rows = inner // count

    got = swapped(projected(other_all, early_weight)[:, : half + state_width])
    kept = projected(own_all, early_weight)
    total_rows = slots + EDGE
    last = groups // 2
    tile = lambda rows, index: pl.BlockSpec((rows, state_width), index)
    whole = lambda shape: pl.BlockSpec(shape, lambda *_: (0,) * len(shape))
    xs, maps, cum, step, payload = pl.pallas_call(
        functools.partial(front_kernel, heads, head_dim, chunk_rows),
        grid=(groups,),
        in_specs=[
            pl.BlockSpec(memory_space=pltpu.SMEM),
            tile(total_rows, lambda g: (0, jnp.minimum(g, last - 1))),
            tile(total_rows, lambda g: (0, jnp.maximum(g - last, 0))),
            tile(total_rows, lambda g: (0, last)),
            tile(total_rows, lambda g: (0, last)),
            tile(total_rows, lambda g: (0, last + 1)),
            tile(8, lambda g: (0, g)),
            whole((8, 2 * state_width)),
            whole((8, state_width)),
        ],
        out_specs=[
            tile(slots, lambda g: (0, g)),
            whole((slots, 2 * state_width)),
            whole((slots, state_width)),
            whole((slots, state_width)),
            whole((count, chunk_rows + 8, state_width)),
        ],
        out_shape=[
            jax.ShapeDtypeStruct((slots, inner), BF16),
            jax.ShapeDtypeStruct((slots, 2 * state_width), BF16),
            jax.ShapeDtypeStruct((slots, state_width), F32),
            jax.ShapeDtypeStruct((slots, state_width), F32),
            jax.ShapeDtypeStruct((count, chunk_rows + 8, state_width), F32),
        ],
        scratch_shapes=[
            pltpu.VMEM((total_rows, state_width), F32),
            pltpu.VMEM((slots, state_width), F32),
            pltpu.VMEM((state_width, slots), BF16),
            pltpu.VMEM((slots, state_width), BF16),
            pltpu.VMEM((slots, state_width), BF16),
        ],
        cost_estimate=pl.CostEstimate(flops=4_000_000_000, bytes_accessed=12_000_000, transcendentals=4_000_000),
        name="front",
    )(scalars, kept, got, kept, got, kept, taps, map_taps, head_rows)

    received = lax.all_to_all(payload, SEQ, 0, 0, tiled=True)
    block_tile = lambda columns, index: pl.BlockSpec((BLOCK, columns), index)
    y = pl.pallas_call(
        functools.partial(inner_kernel, head_dim),
        grid=(capacity, groups),
        in_specs=[
            block_tile(state_width, lambda q, g: (q, g)),
            block_tile(2 * state_width, lambda q, g: (q, 0)),
            block_tile(state_width, lambda q, g: (q, 0)),
            block_tile(state_width, lambda q, g: (q, 0)),
            pl.BlockSpec((8, state_width), lambda q, g: (0, g)),
        ],
        out_specs=block_tile(state_width, lambda q, g: (q, g)),
        out_shape=jax.ShapeDtypeStruct((slots, inner), F32),
        scratch_shapes=[
            pltpu.VMEM((groups, state_width, state_width), F32),
            pltpu.VMEM((BLOCK, BLOCK), F32),
            pltpu.VMEM((state_width, BLOCK), BF16),
            pltpu.VMEM((state_width, BLOCK), F32),
        ],
        cost_estimate=pl.CostEstimate(flops=20_000_000_000, bytes_accessed=14_000_000, transcendentals=12_000_000),
        name="inner",
    )(xs, maps, cum, step, skip)

    gate_weight, _ = lax.optimization_barrier((gate_weight, y))
    got_gate = swapped(projected(other_all[:slots], gate_weight))
    kept_gate = projected(own_rows, gate_weight)

    before = pl.pallas_call(
        functools.partial(prefix_kernel, count, chunk_rows, head_dim),
        in_specs=[pl.BlockSpec(memory_space=pltpu.SMEM), pl.BlockSpec(memory_space=pltpu.VMEM)],
        out_specs=pl.BlockSpec(memory_space=pltpu.VMEM),
        out_shape=jax.ShapeDtypeStruct((count, chunk_rows, state_width), F32),
        scratch_shapes=[pltpu.VMEM((state_width, count), F32)],
        cost_estimate=pl.CostEstimate(flops=2_000_000_000, bytes_accessed=3_000_000, transcendentals=0),
        name="prefix",
    )(lax.axis_index(SEQ).astype(jnp.int32)[None], received)
    state = lax.all_to_all(before, SEQ, 0, 0, tiled=True).reshape(inner, state_width)

    layer_out = pl.pallas_call(
        functools.partial(finish_kernel, head_dim),
        grid=(capacity,),
        in_specs=[
            pl.BlockSpec(memory_space=pltpu.SMEM),
            block_tile(half, lambda q: (q, 0)),
            block_tile(half, lambda q: (q, 0)),
            block_tile(inner, lambda q: (q, 0)),
            block_tile(state_width, lambda q: (q, 1)),
            block_tile(state_width, lambda q: (q, 0)),
            whole((inner, state_width)),
            whole((8, inner)),
        ],
        out_specs=block_tile(inner, lambda q: (q, 0)),
        out_shape=jax.ShapeDtypeStruct((slots, inner), BF16),
        scratch_shapes=[
            pltpu.VMEM((inner, state_width), BF16),
            pltpu.VMEM((inner, state_width), BF16),
            pltpu.VMEM((8, state_width), F32),
            pltpu.VMEM((BLOCK, inner), F32),
        ],
        cost_estimate=pl.CostEstimate(flops=4_000_000_000, bytes_accessed=18_000_000, transcendentals=4_000_000),
        name="finish",
    )(scalars, kept_gate, got_gate, y, maps, cum, state, gain)
    return layer_out[None]


def solution(mesh):
    split = Mesh(
        mesh.devices.reshape(4, 4, 4, mesh.shape["fsdp"]), ("seq_0", "seq_1", "seq_2", "fsdp")
    )
    return jax.shard_map(
        local,
        mesh=split,
        in_specs=(
            P("fsdp", SEQ, None),
            P("fsdp", SEQ, None),
            P(SEQ_FSDP, None),
            P(),
            P(),
            P(),
            P(),
            P(),
            P(),
        ),
        out_specs=P("fsdp", SEQ, None),
        check_vma=False,
    )
```

time: 282 us -> 267 us (0.947)
  Pallas kernels: 3.1 us -> 83.5 us
  other arithmetic: 52.6 us -> 8.11 us
  local copies, waits for them, and re-layouts: 37.5 us -> 11 us
  matrix products: 63.1 us -> 37.4 us
  waiting for transfers between devices: 87.2 us -> 90.8 us
    pallas_call x1 -> x4, Pallas kernels: 3.1 us -> 83.5 us  [the longest x1 41.9 us: local(): pl.pallas_call(functools.partial(inner_kernel, head_dim), grid=(capacity,...]
    dot_general x12 -> x0, matrix products: 30.2 us -> none  [the longest x3 15.9 us: block_terms(): jnp.einsum('hij,jhp->ihp', mixing, head_input, precision=lax.Precision.HIGH)]
    convert_element_type x2 -> x0, other arithmetic: 14.8 us -> none  [the longest x1 8.79 us: local(): layer_out = jnp.where(live_mask, normed, 0.0).astype(BF16)]
    concatenate x3 -> x1, other arithmetic: 13.9 us -> 0.03 us  [local(): jnp.concatenate([conv_weight, conv_bias[None, :]], axis=0)]
    transpose x6 -> x0, local copies, waits for them, and re-layouts: 7.73 us -> none  [the longest x3 4.77 us: carried(): return jnp.exp(cumulative).T[:, :, None] * reach]
    reduce_sum x1 -> x0, other arithmetic: 6.56 us -> none  [local(): jnp.mean(gated * gated, axis=1, keepdims=True) + 1e-05]
    convert_element_type x1 -> x0, local copies, waits for them, and re-layouts: 6.28 us -> none  [local(): layer_out = jnp.where(live_mask, normed, 0.0).astype(BF16)]
    slice x11 -> x6, local copies, waits for them, and re-layouts: 7.37 us -> 1.59 us  [the longest x5 0.99 us: turned_by_core(): second = lax.slice_in_dim(value, middle, 2 * middle, axis=axis)]
  transfers between devices with their start and end apart: 10 -> 10, of which waited for: 6 -> 7; matrix products, arithmetic and copies ran while one was open for 37% -> 18% of each run, Pallas kernels for 1% -> 25%
where the time goes in v2:
time: 267 us; the launch traced here: 263 us
  waiting for transfers between devices  90.8 us (34%)
  Pallas kernels  83.5 us (31%)
  matrix products  37.4 us (14%)
  starting transfers between devices  17.6 us (7%)
  between operations  14.9 us (6%)
  local copies, waits for them, and re-layouts  11 us (4%)
  other arithmetic  8.11 us (3%)
    all_gather x1, waiting for transfers between devices, local(): early_weight = lax.all_gather(paired(mine, other), SEQ, axis=0, tiled=True)  56.8 us
    pallas_call x1, Pallas kernels, local(): pl.pallas_call(functools.partial(inner_kernel, head_dim), grid=(capacity,...  41.9 us
    dot_general x4, matrix products, projected(): return jnp.dot(rows, weight, preferred_element_type=F32).astype(BF16)  37.4 us
    pallas_call x1, Pallas kernels, local(): pl.pallas_call(functools.partial(front_kernel, heads, head_dim, chunk_row...  20.1 us
    pallas_call x1, Pallas kernels, local(): pl.pallas_call(functools.partial(finish_kernel, head_dim), grid=(capacity...  18.4 us
    all_to_all x1, waiting for transfers between devices, local(): received = lax.all_to_all(payload, SEQ, 0, 0, tiled=True)  14.5 us
    all_to_all x1, waiting for transfers between devices, local(): lax.all_to_all(before, SEQ, 0, 0, tiled=True).reshape(inner, state_width)  10.7 us
    all_to_all x1, starting transfers between devices, local(): received = lax.all_to_all(payload, SEQ, 0, 0, tiled=True)  8.99 us
  transfers between devices with their start and end apart: 10, of which 7 were waited for; matrix products, arithmetic and copies ran while one was open for 18% of the time, Pallas kernels for 25%

profile of v2, /device:TPU:0, one launch (start us, length us, event | category | flops | bytes accessed | tf_op | source)
XLA Modules:
  0.0 263.3 jit_solution(2387516943981291742)
XLA Ops:
  6.5 0.8 fusion.7
  7.4 0.9 constant_dynamic-slice_fusion.2
  8.2 1.1 constant_dynamic-slice_fusion.3
  9.4 0.8 broadcast_select_fusion.1
  10.2 0.1 collective-permute-start.2
  10.2 1.3 collective-permute-done.2
  11.5 0.7 maximum_select_fusion
  12.2 0.0 all-gather.5.cloned.1.call-update
  12.2 0.0 all-gather.3.cloned.1.call-start
  12.3 0.2 collective-permute-start
  12.5 1.1 collective-permute-done
  13.6 0.7 maximum_select_fusion.1
  14.3 1.4 fusion.12
  17.0 0.8 dynamic-slice_bitcast_fusion
  17.8 3.5 %collective-permute-start.1 = (bf16[8,2560]{1,0:T(8,128)(2,1)S(1)}, bf16[8,2560]{1,0:T(8,128)(2,1)S(1)}, u32[]{:S(2)}, u32[]{:S(2)}) collective-permute-start(bf16[8,2560]{1,0:T(8,128)(2,1)S(1)} %dynamic-slice_bitcast_fusion), channel_id=1, source_target_pairs={{0,2},{2,4},{4,6},{6,8},{8,10},{10,12},{12,14},{14,16},{16,18},{18... | collective-permute-start | bytes 122888 | tf_op jit(solution)/shard_map/ppermute | solution.py:22
  21.3 1.7 collective-permute-done.1
  23.0 4.4 %pad_maximum_fusion = bf16[776,2560]{1,0:T(8,128)(2,1)} fusion(bf16[8,2560]{1,0:T(8,128)(2,1)S(1)} %collective-permute-done.1, bf16[768,2560]{1,0:T(8,128)(2,1)} %bitcast.22), kind=kLoop, calls=%fused_computation.1 | loop fusion | flops 7946240 | bytes 7946240 | tf_op jit(solution)/shard_map/concatenate | solution.py:335
  27.5 0.6 slice.77.map_conv_ref
  28.1 0.1 fusion.11
  28.1 0.1 broadcast_select_fusion.2
  28.2 0.1 broadcast_in_dim.26
  28.3 0.1 broadcast_in_dim.27
  28.4 0.1 fusion.10
  28.5 0.1 maximum_select_fusion.3
  28.5 0.6 pad.9.head_ref
  29.1 0.7 pad_add_fusion.scalars
  29.8 4.8 %collective-permute-done.3 = bf16[776,2560]{1,0:T(8,128)(2,1)} collective-permute-done((bf16[776,2560]{1,0:T(8,128)(2,1)}, bf16[776,2560]{1,0:T(8,128)(2,1)}, u32[]{:S(2)}, u32[]{:S(2)}) %collective-permute-start.3) | collective-permute-done | bytes 3973152 | tf_op jit(solution)/shard_map/ppermute | solution.py:26
  34.6 56.8 %all-gather.5.cloned.1.call-done = bf16[2560,1448]{1,0:T(8,128)(2,1)} async-done(((bf16[40,1448]{1,0:T(8,128)(2,1)}), bf16[2560,1448]{1,0:T(8,128)(2,1)}) %all-gather.5.cloned.1.call-update) | async-done | bytes 7413776 | tf_op jit(solution)/shard_map/all_gather | solution.py:332
  91.3 10.0 %fusion.13 = bf16[776,1448]{1,0:T(8,128)(2,1)S(1)} fusion(bf16[776,2560]{1,0:T(8,128)(2,1)} %collective-permute-done.3, bf16[2560,1448]{1,0:T(8,128)(2,1)} %all-gather.5.cloned.1.call-done), kind=kOutput, calls=%fused_computation.36 | convolution fusion | flops 5753077760 | bytes 13634176 | tf_op jit(solution)/shard_map/dot_general | solution.py:339
  101.4 0.2 slice.84
  101.5 0.1 collective-permute-start.4
  101.6 0.6 slice_select_fusion.conv_ref
  102.3 1.2 copy-done.1
  103.5 7.7 %convolution_convert_fusion.kept_ref.kept_map_ref.raw_ref = bf16[776,1448]{1,0:T(8,128)(2,1)} fusion(bf16[2560,1448]{1,0:T(8,128)(2,1)S(1)} %copy-done.9, bf16[8,2560]{1,0:T(8,128)(2,1)S(1)} %collective-permute-done.1, bf16[768,2560]{1,0:T(8,128)(2,1)S(1)} %bitcast.23), kind=kOutput, calls=%fused_computation.4 | convolution fusion | flops 5762147840 | bytes 13634176 | tf_op jit(solution)/shard_map/dot_general | solution.py:339
  111.2 1.4 copy-done.10
  112.6 20.1 %front.1 = (bf16[768,2560]{1,0:T(8,128)(2,1)}, bf16[768,256]{1,0:T(8,128)(2,1)}, f32[768,128]{1,0:T(8,128)}, f32[768,128]{1,0:T(8,128)}, f32[64,48,128]{2,1,0:T(8,128)}) custom-call(s32[2]{0:T(128)} %pad_add_fusion.scalars, bf16[776,1448]{1,0:T(8,128)(2,1)} %convolution_convert_fusion.kept_ref.kept_map_ref.raw_ref, bf16[776,1408]{1,0:T(8,128)(2,1)} %copy-done.10, ...), custom_call_target="tpu_custom_call" | custom-call | flops 4000000000 | bytes 12000000 | tf_op jit(solution)/shard_map/front/pallas_call | solution.py:363
  132.7 0.6 broadcast_in_dim.28.skip_ref
  133.4 41.9 %inner.1.y_ref = f32[768,2560]{1,0:T(8,128)} custom-call(bf16[768,2560]{1,0:T(8,128)(2,1)} %get-tuple-element.11.x_ref, bf16[768,256]{1,0:T(8,128)(2,1)} %get-tuple-element.12.maps_ref.c_ref, f32[768,128]{1,0:T(8,128)} %get-tuple-element.13.cum_ref, f32[768,128]{1,0:T(8,128)} %get-tuple-element.14.step_ref, f32[8,2560]{1,0:T(8,128)} %broadcast_in_dim.28.skip_ref), custom_call_target="tpu_custom_call" | custom-call | flops 20000000000 | bytes 14000000 | tf_op jit(solution)/shard_map/inner/pallas_call | solution.py:404
  175.2 9.0 %all-to-all-start = ((f32[64,48,128]{2,1,0:T(8,128)}), f32[64,48,128]{2,1,0:T(8,128)}, u32[]{:S(2)}, u32[]{:S(2)}) async-start(f32[64,48,128]{2,1,0:T(8,128)} %get-tuple-element.16), calls=%async_computation | async-start | bytes 3145728 | tf_op jit(solution)/shard_map/all_to_all | solution.py:402
  184.2 9.8 %fusion.2 = bf16[768,1280]{1,0:T(8,128)(2,1)} fusion(bf16[2560,1280]{1,0:T(8,128)(2,1)} %all-gather.3.cloned.1.call-done, bf16[776,2560]{1,0:T(8,128)(2,1)} %collective-permute-done.3), kind=kOutput, calls=%fused_computation.5 | convolution fusion | flops 5034147840 | bytes 12451840 | tf_op jit(solution)/shard_map/dot_general | solution.py:339
  194.1 14.5 %all-to-all-done.got_ref = f32[64,48,128]{2,1,0:T(8,128)} async-done(((f32[64,48,128]{2,1,0:T(8,128)}), f32[64,48,128]{2,1,0:T(8,128)}, u32[]{:S(2)}, u32[]{:S(2)}) %all-to-all-start) | async-done | bytes 1572896 | tf_op jit(solution)/shard_map/all_to_all | solution.py:402
  208.6 3.1 %prefix.1 = f32[64,40,128]{2,1,0:T(8,128)} custom-call(s32[1]{0:T(128)} %bitcast.9.place_ref, f32[64,48,128]{2,1,0:T(8,128)} %all-to-all-done.got_ref), custom_call_target="tpu_custom_call" | custom-call | flops 2000000000 | bytes 3000000 | tf_op jit(solution)/shard_map/prefix/pallas_call | solution.py:430
  211.7 4.7 %all-to-all-start.1 = ((f32[64,40,128]{2,1,0:T(8,128)}), f32[64,40,128]{2,1,0:T(8,128)S(1)}, u32[]{:S(2)}, u32[]{:S(2)}) async-start(f32[64,40,128]{2,1,0:T(8,128)} %prefix.1), calls=%async_computation.1 | async-start | bytes 2621440 | tf_op jit(solution)/shard_map/all_to_all | solution.py:439
  216.4 9.8 %fusion.5.kept_ref = bf16[768,1280]{1,0:T(8,128)(2,1)} fusion(bf16[2560,1280]{1,0:T(8,128)(2,1)} %all-gather.3.cloned.1.call-done, bf16[1,768,2560]{2,1,0:T(8,128)(2,1)} %param.9), kind=kOutput, calls=%fused_computation.7 | convolution fusion | flops 5034147840 | bytes 12451840 | tf_op jit(solution)/shard_map/dot_general | solution.py:339
  226.2 10.7 %all-to-all-done.1 = f32[64,40,128]{2,1,0:T(8,128)S(1)} async-done(((f32[64,40,128]{2,1,0:T(8,128)}), f32[64,40,128]{2,1,0:T(8,128)S(1)}, u32[]{:S(2)}, u32[]{:S(2)}) %all-to-all-start.1) | async-done | bytes 1310752 | tf_op jit(solution)/shard_map/all_to_all | solution.py:439
  236.9 0.7 broadcast_in_dim.30.gain_ref
  237.6 0.4 copy-done
  238.0 18.4 %finish.1 = bf16[768,2560]{1,0:T(8,128)(2,1)} custom-call(s32[2]{0:T(128)} %pad_add_fusion.scalars, bf16[768,1280]{1,0:T(8,128)(2,1)} %fusion.5.kept_ref, bf16[768,1280]{1,0:T(8,128)(2,1)} %copy-done.2, f32[768,2560]{1,0:T(8,128)} %inner.1.y_ref, bf16[768,256]{1,0:T(8,128)(2,1)} %get-tuple-element.12.maps_ref.c_ref, f32[768,128]{1,0:T(8,128)} %get-tuple-element.13.cum_ref, ...), custom_call_target="tpu_custom_call" | custom-call | flops 4000000000 | bytes 18000000 | tf_op jit(solution)/shard_map/finish/pallas_call | solution.py:441
  (33 shorter events, 0.1 us)
Async XLA Ops:
  6.5 84.8 %all-gather.5.cloned.1.call-start = ((), (), s32[]{:S(2)}) async-start(), calls=%async_computation.3 | async-start | bytes 7987200 | tf_op jit(solution)/shard_map/all_gather | solution.py:332
  10.2 1.3 collective-permute-start.2
  12.2 163.0 %all-gather.3.cloned.1.call-start = ((), (), s32[]{:S(2)}) async-start(), calls=%async_computation.2 | async-start | bytes 6656000 | tf_op jit(solution)/shard_map/all_gather | solution.py:333
  12.3 1.3 collective-permute-start
  17.8 5.2 %collective-permute-start.1 = (bf16[8,2560]{1,0:T(8,128)(2,1)S(1)}, bf16[8,2560]{1,0:T(8,128)(2,1)S(1)}, u32[]{:S(2)}, u32[]{:S(2)}) collective-permute-start(bf16[8,2560]{1,0:T(8,128)(2,1)S(1)} %dynamic-slice_bitcast_fusion), channel_id=1, source_target_pairs={{0,2},{2,4},{4,6},{6,8},{8,10},{10,12},{12,14},{14,16},{16,18},{18... | collective-permute-start | bytes 122888 | tf_op jit(solution)/shard_map/ppermute | solution.py:22
  23.0 4.5 %copy-start.5 = (f32[2816]{0:T(1024)S(1)}, f32[2816]{0:T(1024)}, u32[]{:S(2)}) copy-start(f32[2816]{0:T(1024)} %param.13) | copy-start | bytes 33796
  23.0 4.5 %copy-start.4 = (f32[4,2816]{1,0:T(4,128)S(1)}, f32[4,2816]{1,0:T(4,128)}, u32[]{:S(2)}) copy-start(f32[4,2816]{1,0:T(4,128)} %param.12) | copy-start | bytes 135172
  23.0 5.1 %copy-start.6 = (f32[40]{0:T(128)S(1)}, f32[40]{0:T(128)}, u32[]{:S(2)}) copy-start(f32[40]{0:T(128)} %param.16) | copy-start | bytes 484
  23.0 5.4 %copy-start.7 = (f32[40]{0:T(128)S(1)}, f32[40]{0:T(128)}, u32[]{:S(2)}) copy-start(f32[40]{0:T(128)} %param.15) | copy-start | bytes 484
  23.0 5.4 %copy-start.8 = (f32[40]{0:T(128)S(1)}, f32[40]{0:T(128)}, u32[]{:S(2)}) copy-start(f32[40]{0:T(128)} %param.14) | copy-start | bytes 484
  27.4 7.2 %collective-permute-start.3 = (bf16[776,2560]{1,0:T(8,128)(2,1)}, bf16[776,2560]{1,0:T(8,128)(2,1)}, u32[]{:S(2)}, u32[]{:S(2)}) collective-permute-start(bf16[776,2560]{1,0:T(8,128)(2,1)} %pad_maximum_fusion), channel_id=1, source_target_pairs={{0,1},{1,0},{2,3},{3,2},{4,5},{5,4},{6,7},{7,6},{8,9},{9,8},{10,11... | collective-permute-start | bytes 11919368 | tf_op jit(solution)/shard_map/ppermute | solution.py:26
  91.3 10.9 %copy-start.9 = (bf16[2560,1448]{1,0:T(8,128)(2,1)S(1)}, bf16[2560,1448]{1,0:T(8,128)(2,1)}, u32[]{:S(2)}) copy-start(bf16[2560,1448]{1,0:T(8,128)(2,1)} %all-gather.5.cloned.1.call-done) | copy-start | bytes 22241284
  101.3 2.1 copy-start.1
  101.5 9.7 %collective-permute-start.4 = (bf16[776,1408]{1,0:T(8,128)(2,1)S(1)}, bf16[776,1408]{1,0:T(8,128)(2,1)S(1)}, u32[]{:S(2)}, u32[]{:S(2)}) collective-permute-start(bf16[776,1408]{1,0:T(8,128)(2,1)S(1)} %slice.84), channel_id=1, source_target_pairs={{0,1},{1,0},{2,3},{3,2},{4,5},{5,4},{6,7},{7,6},{8,9},{9,8},{10,11... | collective-permute-start | bytes 6555656 | tf_op jit(solution)/shard_map/ppermute | solution.py:26
  111.2 1.4 copy-start.10
  175.2 33.3 %all-to-all-start = ((f32[64,48,128]{2,1,0:T(8,128)}), f32[64,48,128]{2,1,0:T(8,128)}, u32[]{:S(2)}, u32[]{:S(2)}) async-start(f32[64,48,128]{2,1,0:T(8,128)} %get-tuple-element.16), calls=%async_computation | async-start | bytes 3145728 | tf_op jit(solution)/shard_map/all_to_all | solution.py:402
  184.2 9.8 %copy-start.3 = (f32[2560]{0:T(1024)S(1)}, f32[2560]{0:T(1024)}, u32[]{:S(2)}) copy-start(f32[2560]{0:T(1024)} %param.17) | copy-start | bytes 30724
  194.1 32.1 %collective-permute-start.5 = (bf16[768,1280]{1,0:T(8,128)(2,1)}, bf16[768,1280]{1,0:T(8,128)(2,1)S(1)}, u32[]{:S(2)}, u32[]{:S(2)}) collective-permute-start(bf16[768,1280]{1,0:T(8,128)(2,1)} %fusion.2), channel_id=1, source_target_pairs={{0,1},{1,0},{2,3},{3,2},{4,5},{5,4},{6,7},{7,6},{8,9},{9,8},{10,11... | collective-permute-start | bytes 5898248 | tf_op jit(solution)/shard_map/ppermute | solution.py:26
  211.7 25.3 %all-to-all-start.1 = ((f32[64,40,128]{2,1,0:T(8,128)}), f32[64,40,128]{2,1,0:T(8,128)S(1)}, u32[]{:S(2)}, u32[]{:S(2)}) async-start(f32[64,40,128]{2,1,0:T(8,128)} %prefix.1), calls=%async_computation.1 | async-start | bytes 2621440 | tf_op jit(solution)/shard_map/all_to_all | solution.py:439
  226.2 11.4 %copy-start.2 = (bf16[768,1280]{1,0:T(8,128)(2,1)}, bf16[768,1280]{1,0:T(8,128)(2,1)S(1)}, u32[]{:S(2)}) copy-start(bf16[768,1280]{1,0:T(8,128)(2,1)S(1)} %collective-permute-done.5.got_ref) | copy-start | bytes 5898244
  236.9 1.1 copy-start
Sparse Core Ops, SparseCore 0:
  12.3 78.9 all-gather.4
  94.2 72.3 all-gather.2

commit v3 on v2

v3 whole, which is shorter than its diff:
```python
import functools

import jax
import jax.numpy as jnp
from jax import lax
from jax.experimental import pallas as pl
from jax.experimental.pallas import tpu as pltpu
from jax.sharding import Mesh
from jax.sharding import PartitionSpec as P


BLOCK = 256
EDGE = 8
SEQ_FSDP = ("seq_0", "seq_1", "seq_2", "fsdp")
SEQ = ("seq_0", "seq_1", "seq_2")
F32 = jnp.float32
BF16 = jnp.bfloat16


def passed_along(value, axis, steps):
    count = lax.axis_size(axis)
    leading, last = (max(0, -steps), min(count, count - steps))
    return lax.ppermute(value, axis, [(source, source + steps) for source in range(leading, last)])


def swapped(value):
    return lax.ppermute(value, "fsdp", [(0, 1), (1, 0)])


def pack_kernel(inner, width, core_ref, weight_ref, kept_ref, sent_ref):
    half = inner // 2
    for which, target in ((core_ref[0], kept_ref), (1 - core_ref[0], sent_ref)):
        columns = lambda start, count: weight_ref[:, pl.ds(pl.multiple_of(start, 128), count)]
        target[:, :half] = columns(inner + half * which, half)
        target[:, half : half + width] = columns(2 * inner + width * which, width)
        steps = weight_ref.shape[1] - 2 * inner - 2 * width
        target[:, half + width : half + width + steps] = columns(2 * inner + 2 * width, steps)
        target[:, half + 2 * width :] = columns(half * which, half)


def project_kernel(rows_ref, weight_ref, out_ref):
    out_ref[...] = jnp.dot(
        rows_ref[...], weight_ref[...], preferred_element_type=F32
    ).astype(BF16)


def project(rows, weight, first, count):
    tile = 256
    return pl.pallas_call(
        project_kernel,
        grid=(count // tile,),
        in_specs=[
            pl.BlockSpec(memory_space=pltpu.VMEM),
            pl.BlockSpec((weight.shape[0], tile), lambda j: (0, first // tile + j)),
        ],
        out_specs=pl.BlockSpec((rows.shape[0], tile), lambda j: (0, j)),
        out_shape=jax.ShapeDtypeStruct((rows.shape[0], count), BF16),
        cost_estimate=pl.CostEstimate(
            flops=2 * rows.shape[0] * weight.shape[0] * count, bytes_accessed=14_000_000, transcendentals=0
        ),
        name="project_gate",
    )(rows, weight)


def split_dot(left, right, dims):
    high = right.astype(BF16)
    low = (right - high.astype(F32)).astype(BF16)
    dot = lambda part: lax.dot_general(left, part, (dims, ((), ())), preferred_element_type=F32)
    return dot(high) + dot(low)


def spread(table, lanes):
    index = jnp.broadcast_to(lanes, table.shape)
    return jnp.take_along_axis(table, index, axis=1)


def padded_row(ref, width):
    row = ref[...]
    return jnp.concatenate([row, jnp.zeros((1, width - row.shape[1]), row.dtype)], axis=1)


def lane_ids(shape):
    return lax.broadcasted_iota(jnp.int32, shape, 1)


def front_kernel(
    heads, head_dim, chunk_rows,
    scalars, kept_ref, got_ref, kept_map_ref, got_map_ref, raw_ref, conv_ref, bias_ref, map_conv_ref, map_bias_ref, dt_ref, decay_ref,
    x_ref, maps_ref, cum_ref, step_ref, pay_ref,
    ext, factor, turned, high, low,
):
    part = pl.program_id(0)
    parts = pl.num_programs(0)
    slots, width = cum_ref.shape
    inside = x_ref.shape[1] // width
    chunk = 128

    def fill(ref, at, slot=0):
        ext[slot, :EDGE, :] = ref[slots:, at].astype(F32)
        ext[slot, EDGE:, :] = ref[:slots, at].astype(F32)

    def convolve(taps, bias, start, slot=0):
        first = EDGE - 3 + start
        total = bias + taps[0:1, :] * ext[slot, first : first + chunk, :]
        for offset in range(1, 4):
            total = total + taps[offset : offset + 1, :] * ext[slot, first + offset : first + offset + chunk, :]
        return (total * jax.nn.sigmoid(total)).astype(BF16)

    @pl.when(part == 0)
    def _():
        core, live = scalars[0], scalars[1]
        for which in range(2):
            taps = map_conv_ref[:, which * width : (which + 1) * width]
            bias = map_bias_ref[:, which * width : (which + 1) * width]

            @pl.when(core == which)
            def _():
                fill(kept_map_ref, pl.ds(0, width))

            @pl.when(core != which)
            def _():
                fill(got_map_ref, pl.ds(0, width))

            for start in range(0, slots, chunk):
                value = convolve(taps, bias, start)
                maps_ref[start : start + chunk, which * width : (which + 1) * width] = value
                if which == 0:
                    turned[:, start : start + chunk] = value.astype(F32).T.astype(BF16)
        lanes = lane_ids((slots, width))
        rows = lax.broadcasted_iota(jnp.int32, (slots, width), 0)
        turned_lanes = lane_ids((1, width)) + core * (heads // 2)
        turned_lanes = jnp.where(turned_lanes < heads, turned_lanes, turned_lanes - heads)
        turned_lanes = jnp.where(lane_ids((1, width)) < heads, turned_lanes, 0)
        row = lambda ref: spread(jnp.broadcast_to(padded_row(ref, width), (8, width)), turned_lanes)[0:1, :]
        shifted = spread(raw_ref[:slots, :].astype(F32), turned_lanes) + row(dt_ref)
        step = jnp.maximum(shifted, 0.0) + jnp.log1p(jnp.exp(-jnp.abs(shifted)))
        step = jnp.where((lanes < heads) & (rows < live), step, 0.0)
        step_ref[...] = step
        log_decay = -(step * jnp.where(lane_ids((1, width)) < heads, row(decay_ref), 0.0))
        triangle = (
            lax.broadcasted_iota(jnp.int32, (BLOCK, BLOCK), 0) >= lane_ids((BLOCK, BLOCK))
        ).astype(F32)
        before = jnp.zeros((1, width), F32)
        for lower in range(0, slots, BLOCK):
            cum = jnp.dot(
                triangle,
                log_decay[lower : lower + BLOCK],
                precision=lax.Precision.HIGHEST,
                preferred_element_type=F32,
            )
            cum_ref[lower : lower + BLOCK, :] = cum
            factor[lower : lower + BLOCK, :] = cum + before
            before = before + cum[BLOCK - 1 :, :]
        factor[...] = jnp.exp(before - factor[...]) * step
        pay_ref[:, chunk_rows:, :] = jnp.broadcast_to(
            before[None], (pay_ref.shape[0], pay_ref.shape[1] - chunk_rows, width)
        )

    @pl.when(part < parts // 2)
    def _():
        for k in range(inside):
            fill(kept_ref, pl.ds(k * width, width), k)

    @pl.when(part >= parts // 2)
    def _():
        for k in range(inside):
            fill(got_ref, pl.ds(k * width, width), k)

    for k in range(inside):
        group = part * inside + k
        at = pl.ds(k * width, width)
        odd = k % 2

        lanes = group * (width // head_dim) + lane_ids((1, width)) // head_dim
        taps, bias = conv_ref[:, at], bias_ref[:, at]
        for start in range(0, slots, chunk):
            value = convolve(taps, bias, start, k)
            x_ref[start : start + chunk, at] = value
            weighted = value.astype(F32) * spread(factor[start : start + chunk, :], lanes)
            top = weighted.astype(BF16)
            high[odd, start : start + chunk, :] = top
            low[odd, start : start + chunk, :] = (weighted - top.astype(F32)).astype(BF16)
        state = jnp.dot(turned[...], high[odd], preferred_element_type=F32) + jnp.dot(
            turned[...], low[odd], preferred_element_type=F32
        )
        state = state.T
        pieces = chunk_rows // 8
        for r in range(width // 8):
            place = group * (width // 8) + r
            row = pl.multiple_of(lax.rem(place, pieces) * 8, 8)
            pay_ref[lax.div(place, pieces), pl.ds(row, 8), :] = state[8 * r : 8 * r + 8, :]


def inner_kernel(
    head_dim, heads,
    scalars, x_ref, maps_ref, cum_ref, step_ref, skip_ref, y_ref,
    run, scores, turned, across,
):
    block = pl.program_id(0)
    rows, width = cum_ref.shape
    part = rows // 2
    b, c = maps_ref[:, :width], maps_ref[:, width:]
    scores[...] = lax.dot_general(c, b, (((1,), (1,)), ((), ())), preferred_element_type=F32)
    turned[...] = b.astype(F32).T.astype(BF16)
    across[...] = (cum_ref[...] - jnp.log(step_ref[...])).T

    @pl.when(block == 0)
    def _():
        run[...] = jnp.zeros(run.shape, F32)

    lane = lane_ids((1, width))
    low_lanes = lane_ids((rows, width)) < head_dim
    causal = lax.broadcasted_iota(jnp.int32, (part, part), 0) >= lane_ids((part, part))
    skips = jnp.broadcast_to(padded_row(skip_ref, width), (8, width))

    def each(group, carry):
        at = pl.ds(pl.multiple_of(group * width, width), width)
        first_head = group * (width // head_dim)
        cum = cum_ref[...]
        by_head = [spread(cum, jnp.zeros((1, width), jnp.int32) + first_head + e) for e in range(2)]
        cum_x = jnp.where(low_lanes, by_head[0], by_head[1])
        step_x = spread(step_ref[...], first_head + lane // head_dim)
        x = x_ref[:, at]
        outs = []
        for e in range(2):
            row = across[pl.ds(first_head + e, 1), :]
            column = by_head[e]

            def mixing(i, j):
                exponent = column[i * part : (i + 1) * part, :] - row[:, j * part : (j + 1) * part]
                if i == j:
                    exponent = jnp.where(causal, exponent, -jnp.inf)
                value = jnp.exp(exponent) * scores[i * part : (i + 1) * part, j * part : (j + 1) * part]
                top = value.astype(BF16)
                return top, (value - top.astype(F32)).astype(BF16)

            m00, m10, m11 = mixing(0, 0), mixing(1, 0), mixing(1, 1)
            dot = lambda m, j: jnp.dot(m, x[j * part : (j + 1) * part], preferred_element_type=F32)
            outs.append(
                jnp.concatenate(
                    [
                        dot(m00[0], 0) + dot(m00[1], 0),
                        (dot(m10[0], 0) + dot(m10[1], 0)) + (dot(m11[0], 1) + dot(m11[1], 1)),
                    ],
                    axis=0,
                )
            )
        x32 = x.astype(F32)
        turned_head = first_head + scalars[0] * (heads // 2)
        turned_head = jnp.where(turned_head < heads, turned_head, turned_head - heads)
        skip = spread(skips, turned_head + lane // head_dim)
        state = run[group]
        reach = split_dot(maps_ref[:, width:], state, ((1,), (0,)))
        y_ref[:, at] = (
            jnp.where(low_lanes, outs[0], outs[1]) + jnp.exp(cum_x) * reach + skip[0:1, :] * x32
        )
        end = cum_x[rows - 1 :, :]
        weighted = x32 * (jnp.exp(end - cum_x) * step_x)
        run[group] = jnp.exp(end) * state + split_dot(turned[...], weighted, ((1,), (0,)))
        return carry

    lax.fori_loop(0, run.shape[0], each, 0, unroll=4)


def finish_kernel(
    head_dim,
    scalars, kept_ref, got_ref, y_ref, c_ref, cum_ref, state_ref, gain_ref, out_ref,
    high, low, before, gated,
):
    block = pl.program_id(0)
    rows, inner = y_ref.shape
    width = c_ref.shape[1]
    groups = inner // width

    @pl.when(block == 0)
    def _():
        state = state_ref[...]
        top = state.astype(BF16)
        high[...] = top
        low[...] = (state - top.astype(F32)).astype(BF16)
        before[...] = jnp.zeros(before.shape, F32)

    cum = cum_ref[...] + before[0:1, :]
    before[...] = jnp.broadcast_to(cum[rows - 1 :, :], before.shape)
    reached = jnp.exp(cum)
    c = c_ref[...]
    lane = lane_ids((1, width))

    def half(gate_ref, first):
        def body(k, total):
            group = first + k
            at = pl.ds(pl.multiple_of(group * width, width), width)
            dot = lambda part: lax.dot_general(
                c, part[at, :], (((1,), (1,)), ((), ())), preferred_element_type=F32
            )
            carried = spread(reached, group * (width // head_dim) + lane // head_dim) * (
                dot(high) + dot(low)
            )
            gate = gate_ref[:, pl.ds(pl.multiple_of(k * width, width), width)].astype(F32)
            value = (y_ref[:, at] + carried) * (gate * jax.nn.sigmoid(gate))
            gated[:, at] = value
            return total + value * value

        return body

    total = jnp.zeros((rows, width), F32)
    total = lax.fori_loop(0, groups // 2, half(kept_ref, 0), total, unroll=5)
    total = lax.fori_loop(0, groups // 2, half(got_ref, groups // 2), total, unroll=5)
    scale = lax.rsqrt(jnp.sum(total, axis=1, keepdims=True) / inner + 1e-05)
    live = lax.broadcasted_iota(jnp.int32, (rows, 1), 0) + block * rows < scalars[1]
    shift = scalars[0] * (groups // 2)

    def write(group, _):
        at = pl.ds(pl.multiple_of(group * width, width), width)
        target = lax.rem(group + shift, groups)
        home = pl.ds(pl.multiple_of(target * width, width), width)
        value = gated[:, at] * scale * gain_ref[0:1, home]
        out_ref[:, home] = jnp.where(
            live, value, 0.0
        ).astype(BF16)
        return _

    lax.fori_loop(0, groups, write, 0, unroll=4)


def prefix_kernel(count, rows, head_dim, place_ref, got_ref, out_ref, turned):
    first = lax.div(place_ref[0] * rows, head_dim)
    edge = (first + 1) * head_dim - place_ref[0] * rows
    turned[...] = got_ref[:, rows, :].T
    shape = (rows, count)
    decays = jnp.exp(
        jnp.where(
            lax.broadcasted_iota(jnp.int32, shape, 0) < edge,
            jnp.broadcast_to(turned[pl.ds(first, 1), :], shape),
            jnp.broadcast_to(turned[pl.ds(first + 1, 1), :], shape),
        )
    )
    state = jnp.zeros((rows, got_ref.shape[2]), F32)
    for source in range(count):
        out_ref[source] = state
        if source < count - 1:
            factor = jnp.broadcast_to(decays[:, source : source + 1], state.shape)
            state = state * factor + got_ref[source, :rows, :]


def local(
    tokens, bounds, in_weight, conv_weight, conv_bias, dt_bias, decay_rate, skip_gain, norm_gain
):
    slots = tokens.shape[1]
    inner = norm_gain.shape[0]
    state_width = (conv_bias.shape[0] - inner) // 2
    heads = decay_rate.shape[0]
    head_dim = inner // heads
    kernel = conv_weight.shape[0]
    capacity = slots // BLOCK
    half = inner // 2
    core = lax.axis_index("fsdp")
    early_width = [4 * state_width] * 3
    early_total = sum(early_width)
    core_scalar = core.astype(jnp.int32)[None]
    part_shape = jax.ShapeDtypeStruct((in_weight.shape[0], early_total + half), BF16)
    kept_part, sent_part = pl.pallas_call(
        functools.partial(pack_kernel, inner, state_width),
        in_specs=[pl.BlockSpec(memory_space=pltpu.SMEM), pl.BlockSpec(memory_space=pltpu.VMEM)],
        out_specs=[pl.BlockSpec(memory_space=pltpu.VMEM)] * 2,
        out_shape=[part_shape] * 2,
        name="pack",
    )(core_scalar, in_weight)
    received = swapped(sent_part)
    shard = jnp.where(
        core == 0,
        jnp.concatenate([kept_part, received], axis=0),
        jnp.concatenate([received, kept_part], axis=0),
    )
    weight = lax.all_gather(shard, SEQ, axis=0, tiled=True)
    own_rows = tokens[0]
    shard_blocks = bounds[0, 0, 1] - bounds[0, 0, 0]
    edge = lax.dynamic_slice_in_dim(own_rows, shard_blocks * BLOCK - EDGE, EDGE, 0)
    own_all = jnp.concatenate([own_rows, passed_along(edge, SEQ, 1)], axis=0)
    other_all = swapped(own_all)

    def projected(rows, first, count):
        part = lax.slice_in_dim(weight, first, first + count, axis=1)
        return jnp.dot(rows, part, preferred_element_type=F32).astype(BF16)

    groups = inner // state_width
    scalars = jnp.stack([core.astype(jnp.int32), shard_blocks * BLOCK])
    bias_row, gain_row = conv_bias[None, :], norm_gain[None, :]
    dt_row, decay_row, skip_row = dt_bias[None, :], decay_rate[None, :], skip_gain[None, :]
    count = lax.axis_size(SEQ)
    chunk_rows = inner // count

    total_rows = slots + EDGE
    theirs = projected(other_all, 0, early_total)
    got = swapped(theirs)
    kept = projected(own_all, 0, early_total)
    last = groups // 2
    tile = lambda rows, index: pl.BlockSpec((rows, state_width), index)
    whole = lambda shape: pl.BlockSpec(shape, lambda *_: (0,) * len(shape))
    parts = 4
    wide = inner // parts
    turn = lambda p, c: lax.rem(p + c[0] * (parts // 2), parts)
    broad = lambda rows, index: pl.BlockSpec((rows, wide), index)
    xs, maps, cum, step, payload = pl.pallas_call(
        functools.partial(front_kernel, heads, head_dim, chunk_rows),
        grid_spec=pltpu.PrefetchScalarGridSpec(
            num_scalar_prefetch=1,
            grid=(parts,),
            in_specs=[
            broad(total_rows, lambda p, c: (0, jnp.minimum(p, parts // 2 - 1))),
            broad(total_rows, lambda p, c: (0, jnp.maximum(p - parts // 2, 0))),
            tile(total_rows, lambda g, c: (0, last)),
            tile(total_rows, lambda g, c: (0, last)),
            tile(total_rows, lambda g, c: (0, last + 1)),
            broad(kernel, lambda p, c: (0, turn(p, c))),
            broad(1, lambda p, c: (0, turn(p, c))),
            pl.BlockSpec((kernel, 2 * state_width), lambda g, c: (0, groups // 2)),
            pl.BlockSpec((1, 2 * state_width), lambda g, c: (0, groups // 2)),
            whole((1, heads)),
            whole((1, heads)),
        ],
        out_specs=[
            broad(slots, lambda p, c: (0, p)),
            whole((slots, 2 * state_width)),
            whole((slots, state_width)),
            whole((slots, state_width)),
            whole((count, chunk_rows + 8, state_width)),
        ],
            scratch_shapes=[
            pltpu.VMEM((groups // parts, total_rows, state_width), F32),
            pltpu.VMEM((slots, state_width), F32),
            pltpu.VMEM((state_width, slots), BF16),
            pltpu.VMEM((2, slots, state_width), BF16),
            pltpu.VMEM((2, slots, state_width), BF16),
        ],
        ),
        out_shape=[
            jax.ShapeDtypeStruct((slots, inner), BF16),
            jax.ShapeDtypeStruct((slots, 2 * state_width), BF16),
            jax.ShapeDtypeStruct((slots, state_width), F32),
            jax.ShapeDtypeStruct((slots, state_width), F32),
            jax.ShapeDtypeStruct((count, chunk_rows + 8, state_width), F32),
        ],
        cost_estimate=pl.CostEstimate(flops=4_000_000_000, bytes_accessed=12_000_000, transcendentals=4_000_000),
        name="front",
    )(scalars, kept, got, kept, got, kept, conv_weight, bias_row, conv_weight, bias_row, dt_row, decay_row)

    received = lax.all_to_all(payload, SEQ, 0, 0, tiled=True)
    block_tile = lambda columns, index: pl.BlockSpec((BLOCK, columns), index)
    y = pl.pallas_call(
        functools.partial(inner_kernel, head_dim, heads),
        grid=(capacity,),
        in_specs=[
            pl.BlockSpec(memory_space=pltpu.SMEM),
            block_tile(inner, lambda q: (q, 0)),
            block_tile(2 * state_width, lambda q: (q, 0)),
            block_tile(state_width, lambda q: (q, 0)),
            block_tile(state_width, lambda q: (q, 0)),
            whole((1, heads)),
        ],
        out_specs=block_tile(inner, lambda q: (q, 0)),
        out_shape=jax.ShapeDtypeStruct((slots, inner), F32),
        scratch_shapes=[
            pltpu.VMEM((groups, state_width, state_width), F32),
            pltpu.VMEM((BLOCK, BLOCK), F32),
            pltpu.VMEM((state_width, BLOCK), BF16),
            pltpu.VMEM((state_width, BLOCK), F32),
        ],
        cost_estimate=pl.CostEstimate(flops=20_000_000_000, bytes_accessed=14_000_000, transcendentals=12_000_000),
        name="inner",
    )(scalars, xs, maps, cum, step, skip_row)

    received, y = lax.optimization_barrier((received, y))
    before = pl.pallas_call(
        functools.partial(prefix_kernel, count, chunk_rows, head_dim),
        in_specs=[pl.BlockSpec(memory_space=pltpu.SMEM), pl.BlockSpec(memory_space=pltpu.VMEM)],
        out_specs=pl.BlockSpec(memory_space=pltpu.VMEM),
        out_shape=jax.ShapeDtypeStruct((count, chunk_rows, state_width), F32),
        scratch_shapes=[pltpu.VMEM((state_width, count), F32)],
        cost_estimate=pl.CostEstimate(flops=2_000_000_000, bytes_accessed=3_000_000, transcendentals=0),
        name="prefix",
    )(lax.axis_index(SEQ).astype(jnp.int32)[None], received)
    weight, _ = lax.optimization_barrier((weight, before))
    theirs_gate = project(other_all, weight, early_total, half)
    kept_gate = project(own_all, weight, early_total, half)
    got_gate = swapped(theirs_gate)

    state = lax.all_to_all(before, SEQ, 0, 0, tiled=True).reshape(inner, state_width)

    layer_out = pl.pallas_call(
        functools.partial(finish_kernel, head_dim),
        grid=(capacity,),
        in_specs=[
            pl.BlockSpec(memory_space=pltpu.SMEM),
            block_tile(half, lambda q: (q, 0)),
            block_tile(half, lambda q: (q, 0)),
            block_tile(inner, lambda q: (q, 0)),
            block_tile(state_width, lambda q: (q, 1)),
            block_tile(state_width, lambda q: (q, 0)),
            whole((inner, state_width)),
            whole((1, inner)),
        ],
        out_specs=block_tile(inner, lambda q: (q, 0)),
        out_shape=jax.ShapeDtypeStruct((slots, inner), BF16),
        scratch_shapes=[
            pltpu.VMEM((inner, state_width), BF16),
            pltpu.VMEM((inner, state_width), BF16),
            pltpu.VMEM((8, state_width), F32),
            pltpu.VMEM((BLOCK, inner), F32),
        ],
        cost_estimate=pl.CostEstimate(flops=4_000_000_000, bytes_accessed=18_000_000, transcendentals=4_000_000),
        name="finish",
    )(scalars, kept_gate, got_gate, y, maps, cum, state, gain_row)
    return layer_out[None]


def solution(mesh):
    split = Mesh(
        mesh.devices.reshape(4, 4, 4, mesh.shape["fsdp"]), ("seq_0", "seq_1", "seq_2", "fsdp")
    )
    return jax.shard_map(
        local,
        mesh=split,
        in_specs=(
            P("fsdp", SEQ, None),
            P("fsdp", SEQ, None),
            P(SEQ_FSDP, None),
            P(),
            P(),
            P(),
            P(),
            P(),
            P(),
        ),
        out_specs=P("fsdp", SEQ, None),
        check_vma=False,
    )
```

time: 267 us -> 249 us (0.933)
  matrix products: 37.4 us -> 21.7 us
  waiting for transfers between devices: 90.8 us -> 104 us
  Pallas kernels: 83.5 us -> 73 us
  other arithmetic: 8.11 us -> 4.75 us
    all_gather x2 -> x1, waiting for transfers between devices: 56.8 us -> 79.5 us  [local(): weight = lax.all_gather(shard, SEQ, axis=0, tiled=True)]
    dot_general x4 -> x2, matrix products: 37.4 us -> 21.7 us  [projected(): return jnp.dot(rows, part, preferred_element_type=F32).astype(BF16)]
    all_to_all x1, waiting for transfers between devices: 14.5 us -> 2.85 us  [local(): received = lax.all_to_all(payload, SEQ, 0, 0, tiled=True)]
    pallas_call x1, Pallas kernels: 18.4 us -> 11.6 us  [local(): pl.pallas_call(functools.partial(finish_kernel, head_dim), grid=(capacity...]
    pallas_call x1, Pallas kernels: 20.1 us -> 14.4 us  [local(): pl.pallas_call(functools.partial(front_kernel, heads, head_dim, chunk_row...]
    unnamed x22 -> x14, local copies, waits for them, and re-layouts: 3.09 us -> 6.23 us
    pallas_call x1 -> x4, Pallas kernels: 41.9 us -> 43.9 us  [the longest x1 22.4 us: local(): pl.pallas_call(functools.partial(inner_kernel, head_dim, heads), grid=(ca...]
    ppermute x5 -> x4, waiting for transfers between devices: 7.14 us -> 8.54 us  [swapped(): return lax.ppermute(value, 'fsdp', [(0, 1), (1, 0)])]
  transfers between devices with their start and end apart: 10 -> 8, of which waited for: 7 -> 6; matrix products, arithmetic and copies ran while one was open for 18% -> 7% of each run, Pallas kernels for 25% -> 13%
where the time goes in v3:
time: 249 us; the launch traced here: 248 us
  waiting for transfers between devices  104 us (42%)
  Pallas kernels  73 us (29%)
  matrix products  21.7 us (9%)
  starting transfers between devices  19.6 us (8%)
  between operations  14.8 us (6%)
  local copies, waits for them, and re-layouts  9.59 us (4%)
  other arithmetic  4.75 us (2%)
    all_gather x1, waiting for transfers between devices, local(): weight = lax.all_gather(shard, SEQ, axis=0, tiled=True)  79.5 us
    pallas_call x1, Pallas kernels, local(): pl.pallas_call(functools.partial(inner_kernel, head_dim, heads), grid=(ca...  22.4 us
    dot_general x2, matrix products, projected(): return jnp.dot(rows, part, preferred_element_type=F32).astype(BF16)  21.7 us
    pallas_call x2, Pallas kernels, project(): pl.pallas_call(project_kernel, grid=(count // tile,), in_specs=[pl.BlockS...  19.8 us
    pallas_call x1, Pallas kernels, local(): pl.pallas_call(functools.partial(front_kernel, heads, head_dim, chunk_row...  14.4 us
    all_to_all x1, waiting for transfers between devices, local(): lax.all_to_all(before, SEQ, 0, 0, tiled=True).reshape(inner, state_width)  11.9 us
    pallas_call x1, Pallas kernels, local(): pl.pallas_call(functools.partial(finish_kernel, head_dim), grid=(capacity...  11.6 us
    all_to_all x1, starting transfers between devices, local(): received = lax.all_to_all(payload, SEQ, 0, 0, tiled=True)  8.79 us
  transfers between devices with their start and end apart: 8, of which 6 were waited for; matrix products, arithmetic and copies ran while one was open for 7% of the time, Pallas kernels for 13%

profile of v3, /device:TPU:0, one launch (start us, length us, event | category | flops | bytes accessed | tf_op | source)
XLA Modules:
  0.0 247.9 jit_solution(9199495287053997931)
XLA Ops:
  6.5 0.0 all-gather.2.cloned.1.call-start
  6.5 1.7 pack.1
  8.2 0.0 collective-permute-start.1
  8.2 1.6 collective-permute-done.1
  9.8 1.8 maximum_select_fusion
  11.5 0.0 all-gather.2.cloned.1.call-update
  11.6 1.4 fusion.10
  14.2 0.8 dynamic-slice_bitcast_fusion
  15.0 3.5 %collective-permute-start = (bf16[8,2560]{1,0:T(8,128)(2,1)S(1)}, bf16[8,2560]{1,0:T(8,128)(2,1)S(1)}, u32[]{:S(2)}, u32[]{:S(2)}) collective-permute-start(bf16[8,2560]{1,0:T(8,128)(2,1)S(1)} %dynamic-slice_bitcast_fusion), channel_id=1, source_target_pairs={{0,2},{2,4},{4,6},{6,8},{8,10},{10,12},{12,14},{14,16},{16,18},{18... | collective-permute-start | bytes 122888 | tf_op jit(solution)/shard_map/ppermute | solution.py:23
  18.5 1.7 collective-permute-done
  20.2 2.4 pad_maximum_fusion.rows_ref
  22.6 0.0 copy-start
  22.6 1.9 copy-done
  24.5 0.0 copy-start.4
  24.5 0.0 collective-permute-start.2
  24.5 7.0 %collective-permute-done.2.rows_ref = bf16[776,2560]{1,0:T(8,128)(2,1)} collective-permute-done((bf16[776,2560]{1,0:T(8,128)(2,1)S(1)}, bf16[776,2560]{1,0:T(8,128)(2,1)}, u32[]{:S(2)}, u32[]{:S(2)}) %collective-permute-start.2) | collective-permute-done | bytes 3973152 | tf_op jit(solution)/shard_map/ppermute | solution.py:27
  31.5 79.5 %all-gather.2.cloned.1.call-done.weight_ref = bf16[2560,2816]{1,0:T(8,128)(2,1)} async-done(((bf16[40,2816]{1,0:T(8,128)(2,1)}), bf16[2560,2816]{1,0:T(8,128)(2,1)}) %all-gather.2.cloned.1.call-update) | async-done | bytes 14417936 | tf_op jit(solution)/shard_map/all_gather | solution.py:375
  111.0 10.9 %fusion.7 = bf16[776,1536]{1,0:T(8,128)(2,1)} fusion(bf16[776,2560]{1,0:T(8,128)(2,1)} %collective-permute-done.2.rows_ref, bf16[2560,2816]{1,0:T(8,128)(2,1)} %all-gather.2.cloned.1.call-done.weight_ref), kind=kOutput, calls=%fused_computation.6 | convolution fusion | flops 6103904256 | bytes 14221312 | tf_op jit(solution)/shard_map/dot_general | solution.py:384
  121.9 0.0 collective-permute-start.3
  121.9 0.0 copy-done.4
  121.9 0.6 broadcast_in_dim.23.bias_ref.map_bias_ref
  122.5 0.6 pad_add_fusion.scalars
  123.1 10.9 %fusion.4.kept_ref.kept_map_ref.raw_ref = bf16[776,1536]{1,0:T(8,128)(2,1)} fusion(bf16[2560,2816]{1,0:T(8,128)(2,1)} %all-gather.2.cloned.1.call-done.weight_ref, bf16[8,2560]{1,0:T(8,128)(2,1)S(1)} %collective-permute-done, bf16[768,2560]{1,0:T(8,128)(2,1)} %bitcast.16), kind=kOutput, calls=%fused_computation.5 | convolution fusion | flops 6111850496 | bytes 14221312 | tf_op jit(solution)/shard_map/dot_general | solution.py:384
  134.0 0.0 collective-permute-done.3.got_ref.got_map_ref
  134.0 0.0 copy-start.6
  134.0 1.4 copy-done.6
  135.4 14.4 %front.1 = (bf16[768,2560]{1,0:T(8,128)(2,1)}, bf16[768,256]{1,0:T(8,128)(2,1)}, f32[768,128]{1,0:T(8,128)}, f32[768,128]{1,0:T(8,128)}, f32[64,48,128]{2,1,0:T(8,128)}) custom-call(s32[2]{0:T(128)} %pad_add_fusion.scalars, bf16[776,1536]{1,0:T(8,128)(2,1)} %fusion.4.kept_ref.kept_map_ref.raw_ref, bf16[776,1536]{1,0:T(8,128)(2,1)} %copy-done.6, ...), custom_call_target="tpu_custom_call" | custom-call | flops 4000000000 | bytes 12000000 | tf_op jit(solution)/shard_map/front/pallas_call | solution.py:404
  149.9 8.8 %all-to-all-start = ((f32[64,48,128]{2,1,0:T(8,128)}), f32[64,48,128]{2,1,0:T(8,128)S(1)}, u32[]{:S(2)}, u32[]{:S(2)}) async-start(f32[64,48,128]{2,1,0:T(8,128)} %get-tuple-element.17), calls=%async_computation | async-start | bytes 3145728 | tf_op jit(solution)/shard_map/all_to_all | solution.py:448
  158.7 22.4 %inner.1.y_ref = f32[768,2560]{1,0:T(8,128)} custom-call(s32[2]{0:T(128)} %pad_add_fusion.scalars, bf16[768,2560]{1,0:T(8,128)(2,1)} %get-tuple-element.18.x_ref, bf16[768,256]{1,0:T(8,128)(2,1)} %get-tuple-element.19.maps_ref.c_ref, f32[768,128]{1,0:T(8,128)} %get-tuple-element.20.cum_ref, f32[768,128]{1,0:T(8,128)} %get-tuple-element.21.step_ref, ...), custom_call_target="tpu_custom_call" | custom-call | flops 20000000000 | bytes 14000000 | tf_op jit(solution)/shard_map/inner/pallas_call | solution.py:450
  181.1 2.8 %all-to-all-done.got_ref = f32[64,48,128]{2,1,0:T(8,128)S(1)} async-done(((f32[64,48,128]{2,1,0:T(8,128)}), f32[64,48,128]{2,1,0:T(8,128)S(1)}, u32[]{:S(2)}, u32[]{:S(2)}) %all-to-all-start) | async-done | bytes 1572896 | tf_op jit(solution)/shard_map/all_to_all | solution.py:448
  183.9 0.0 copy-start.3
  183.9 1.1 copy-done.3
  185.1 3.1 %prefix.1 = f32[64,40,128]{2,1,0:T(8,128)} custom-call(s32[1]{0:T(128)} %bitcast.6.place_ref, f32[64,48,128]{2,1,0:T(8,128)} %copy-done.3), custom_call_target="tpu_custom_call" | custom-call | flops 2000000000 | bytes 3000000 | tf_op jit(solution)/shard_map/prefix/pallas_call | solution.py:474
  188.2 0.0 copy-start.5
  188.2 9.9 %project_gate.3 = bf16[776,1280]{1,0:T(8,128)(2,1)} custom-call(bf16[776,2560]{1,0:T(8,128)(2,1)} %collective-permute-done.2.rows_ref, bf16[2560,2816]{1,0:T(8,128)(2,1)} %all-gather.2.cloned.1.call-done.weight_ref), custom_call_target="tpu_custom_call" | custom-call | flops 5085593600 | bytes 14000000 | tf_op jit(solution)/shard_map/project_gate/pallas_call | solution.py:49
  198.0 0.0 collective-permute-start.4
  198.0 7.3 %all-to-all-start.1 = ((f32[64,40,128]{2,1,0:T(8,128)}), f32[64,40,128]{2,1,0:T(8,128)S(1)}, u32[]{:S(2)}, u32[]{:S(2)}) async-start(f32[64,40,128]{2,1,0:T(8,128)} %prefix.1), calls=%async_computation.1 | async-start | bytes 2621440 | tf_op jit(solution)/shard_map/all_to_all | solution.py:488
  205.4 0.0 copy-done.5
  205.4 0.6 broadcast_in_dim.27.gain_ref
  206.0 9.9 %project_gate.2.kept_ref = bf16[776,1280]{1,0:T(8,128)(2,1)} custom-call(bf16[776,2560]{1,0:T(8,128)(2,1)} %copy-done, bf16[2560,2816]{1,0:T(8,128)(2,1)} %all-gather.2.cloned.1.call-done.weight_ref), custom_call_target="tpu_custom_call" | custom-call | flops 5085593600 | bytes 14000000 | tf_op jit(solution)/shard_map/project_gate/pallas_call | solution.py:49
  215.9 11.9 %all-to-all-done.1 = f32[64,40,128]{2,1,0:T(8,128)S(1)} async-done(((f32[64,40,128]{2,1,0:T(8,128)}), f32[64,40,128]{2,1,0:T(8,128)S(1)}, u32[]{:S(2)}, u32[]{:S(2)}) %all-to-all-start.1) | async-done | bytes 1310752 | tf_op jit(solution)/shard_map/all_to_all | solution.py:488
  227.8 0.0 copy-start.1
  227.8 0.0 collective-permute-done.4.got_ref
  227.8 0.0 copy-start.2
  227.8 1.2 copy-done.1
  229.0 0.5 copy-done.2
  229.5 11.6 %finish.1 = bf16[768,2560]{1,0:T(8,128)(2,1)} custom-call(s32[2]{0:T(128)} %pad_add_fusion.scalars, bf16[776,1280]{1,0:T(8,128)(2,1)} %project_gate.2.kept_ref, bf16[776,1280]{1,0:T(8,128)(2,1)} %copy-done.2, f32[768,2560]{1,0:T(8,128)} %inner.1.y_ref, bf16[768,256]{1,0:T(8,128)(2,1)} %get-tuple-element.19.maps_ref.c_ref, ...), custom_call_target="tpu_custom_call" | custom-call | flops 4000000000 | bytes 18000000 | tf_op jit(solution)/shard_map/finish/pallas_call | solution.py:490
Async XLA Ops:
  6.5 104.5 %all-gather.2.cloned.1.call-start = ((), (), s32[]{:S(2)}) async-start(), calls=%async_computation.2 | async-start | bytes 14643200 | tf_op jit(solution)/shard_map/all_gather | solution.py:375
  8.2 1.6 collective-permute-start.1
  15.0 5.2 %collective-permute-start = (bf16[8,2560]{1,0:T(8,128)(2,1)S(1)}, bf16[8,2560]{1,0:T(8,128)(2,1)S(1)}, u32[]{:S(2)}, u32[]{:S(2)}) collective-permute-start(bf16[8,2560]{1,0:T(8,128)(2,1)S(1)} %dynamic-slice_bitcast_fusion), channel_id=1, source_target_pairs={{0,2},{2,4},{4,6},{6,8},{8,10},{10,12},{12,14},{14,16},{16,18},{18... | collective-permute-start | bytes 122888 | tf_op jit(solution)/shard_map/ppermute | solution.py:23
  22.6 2.0 copy-start
  24.5 97.4 %copy-start.4 = (f32[2816]{0:T(1024)S(1)}, f32[2816]{0:T(1024)}, u32[]{:S(2)}) copy-start(f32[2816]{0:T(1024)} %param.13) | copy-start | bytes 33796
  24.5 7.0 %collective-permute-start.2 = (bf16[776,2560]{1,0:T(8,128)(2,1)S(1)}, bf16[776,2560]{1,0:T(8,128)(2,1)}, u32[]{:S(2)}, u32[]{:S(2)}) collective-permute-start(bf16[776,2560]{1,0:T(8,128)(2,1)S(1)} %pad_maximum_fusion.rows_ref), channel_id=1, source_target_pairs={{0,1},{1,0},{2,3},{3,2},{4,5},{5,4},{6,7},{7,6},{8,9},{9,8},{10,11... | collective-permute-start | bytes 11919368 | tf_op jit(solution)/shard_map/ppermute | solution.py:27
  121.9 12.1 %collective-permute-start.3 = (bf16[776,1536]{1,0:T(8,128)(2,1)}, bf16[776,1536]{1,0:T(8,128)(2,1)S(1)}, u32[]{:S(2)}, u32[]{:S(2)}) collective-permute-start(bf16[776,1536]{1,0:T(8,128)(2,1)} %fusion.7), channel_id=1, source_target_pairs={{0,1},{1,0},{2,3},{3,2},{4,5},{5,4},{6,7},{7,6},{8,9},{9,8},{10,11... | collective-permute-start | bytes 7151624 | tf_op jit(solution)/shard_map/ppermute | solution.py:27
  134.0 1.4 copy-start.6
  149.9 34.0 %all-to-all-start = ((f32[64,48,128]{2,1,0:T(8,128)}), f32[64,48,128]{2,1,0:T(8,128)S(1)}, u32[]{:S(2)}, u32[]{:S(2)}) async-start(f32[64,48,128]{2,1,0:T(8,128)} %get-tuple-element.17), calls=%async_computation | async-start | bytes 3145728 | tf_op jit(solution)/shard_map/all_to_all | solution.py:448
  183.9 1.1 copy-start.3
  188.2 17.2 %copy-start.5 = (f32[2560]{0:T(1024)S(1)}, f32[2560]{0:T(1024)}, u32[]{:S(2)}) copy-start(f32[2560]{0:T(1024)} %param.17) | copy-start | bytes 30724
  198.0 29.8 %collective-permute-start.4 = (bf16[776,1280]{1,0:T(8,128)(2,1)}, bf16[776,1280]{1,0:T(8,128)(2,1)S(1)}, u32[]{:S(2)}, u32[]{:S(2)}) collective-permute-start(bf16[776,1280]{1,0:T(8,128)(2,1)} %project_gate.3), channel_id=1, source_target_pairs={{0,1},{1,0},{2,3},{3,2},{4,5},{5,4},{6,7},{7,6},{8,9},{9,8},{10,11... | collective-permute-start | bytes 5959688 | tf_op jit(solution)/shard_map/ppermute | solution.py:27
  198.0 29.8 %all-to-all-start.1 = ((f32[64,40,128]{2,1,0:T(8,128)}), f32[64,40,128]{2,1,0:T(8,128)S(1)}, u32[]{:S(2)}, u32[]{:S(2)}) async-start(f32[64,40,128]{2,1,0:T(8,128)} %prefix.1), calls=%async_computation.1 | async-start | bytes 2621440 | tf_op jit(solution)/shard_map/all_to_all | solution.py:488
  227.8 1.2 copy-start.1
  227.8 1.7 copy-start.2
Sparse Core Ops, SparseCore 0:
  11.7 99.2 all-gather.1

commit v4 on v3

--- a/solution.py
+++ b/solution.py
@@ -85,14 +85,15 @@
 
 def front_kernel(
     heads, head_dim, chunk_rows,
-    scalars, kept_ref, got_ref, kept_map_ref, got_map_ref, raw_ref, conv_ref, bias_ref, map_conv_ref, map_bias_ref, dt_ref, decay_ref,
+    scalars, kept_ref, got_ref, conv_ref, bias_ref, map_conv_ref, map_bias_ref, dt_ref, decay_ref,
     x_ref, maps_ref, cum_ref, step_ref, pay_ref,
     ext, factor, turned, high, low,
 ):
     part = pl.program_id(0)
     parts = pl.num_programs(0)
     slots, width = cum_ref.shape
-    inside = x_ref.shape[1] // width
+    wide = x_ref.shape[1]
+    inside, half = wide // width, wide * parts // 2
     chunk = 128
 
     def fill(ref, at, slot=0):
@@ -115,11 +116,11 @@
 
             @pl.when(core == which)
             def _():
-                fill(kept_map_ref, pl.ds(0, width))
+                fill(kept_ref, pl.ds(half, width))
 
             @pl.when(core != which)
             def _():
-                fill(got_map_ref, pl.ds(0, width))
+                fill(got_ref, pl.ds(half, width))
 
             for start in range(0, slots, chunk):
                 value = convolve(taps, bias, start)
@@ -132,7 +133,7 @@
         turned_lanes = jnp.where(turned_lanes < heads, turned_lanes, turned_lanes - heads)
         turned_lanes = jnp.where(lane_ids((1, width)) < heads, turned_lanes, 0)
         row = lambda ref: spread(jnp.broadcast_to(padded_row(ref, width), (8, width)), turned_lanes)[0:1, :]
-        shifted = spread(raw_ref[:slots, :].astype(F32), turned_lanes) + row(dt_ref)
+        shifted = spread(kept_ref[:slots, half + width : half + 2 * width].astype(F32), turned_lanes) + row(dt_ref)
         step = jnp.maximum(shifted, 0.0) + jnp.log1p(jnp.exp(-jnp.abs(shifted)))
         step = jnp.where((lanes < heads) & (rows < live), step, 0.0)
         step_ref[...] = step
@@ -159,12 +160,12 @@
     @pl.when(part < parts // 2)
     def _():
         for k in range(inside):
-            fill(kept_ref, pl.ds(k * width, width), k)
+            fill(kept_ref, pl.ds(pl.multiple_of(part * wide + k * width, width), width), k)
 
     @pl.when(part >= parts // 2)
     def _():
         for k in range(inside):
-            fill(got_ref, pl.ds(k * width, width), k)
+            fill(got_ref, pl.ds(pl.multiple_of((part - parts // 2) * wide + k * width, width), width), k)
 
     for k in range(inside):
         group = part * inside + k
@@ -387,6 +388,9 @@
     scalars = jnp.stack([core.astype(jnp.int32), shard_blocks * BLOCK])
     bias_row, gain_row = conv_bias[None, :], norm_gain[None, :]
     dt_row, decay_row, skip_row = dt_bias[None, :], decay_rate[None, :], skip_gain[None, :]
+    own_all, bias_row, gain_row, scalars = lax.optimization_barrier(
+        (own_all, bias_row, gain_row, scalars)
+    )
     count = lax.axis_size(SEQ)
     chunk_rows = inner // count
 
@@ -394,8 +398,6 @@
     theirs = projected(other_all, 0, early_total)
     got = swapped(theirs)
     kept = projected(own_all, 0, early_total)
-    last = groups // 2
-    tile = lambda rows, index: pl.BlockSpec((rows, state_width), index)
     whole = lambda shape: pl.BlockSpec(shape, lambda *_: (0,) * len(shape))
     parts = 4
     wide = inner // parts
@@ -407,11 +409,8 @@
             num_scalar_prefetch=1,
             grid=(parts,),
             in_specs=[
-            broad(total_rows, lambda p, c: (0, jnp.minimum(p, parts // 2 - 1))),
-            broad(total_rows, lambda p, c: (0, jnp.maximum(p - parts // 2, 0))),
-            tile(total_rows, lambda g, c: (0, last)),
-            tile(total_rows, lambda g, c: (0, last)),
-            tile(total_rows, lambda g, c: (0, last + 1)),
+            pl.BlockSpec(memory_space=pltpu.VMEM),
+            pl.BlockSpec(memory_space=pltpu.VMEM),
             broad(kernel, lambda p, c: (0, turn(p, c))),
             broad(1, lambda p, c: (0, turn(p, c))),
             pl.BlockSpec((kernel, 2 * state_width), lambda g, c: (0, groups // 2)),
@@ -442,8 +441,9 @@
             jax.ShapeDtypeStruct((count, chunk_rows + 8, state_width), F32),
         ],
         cost_estimate=pl.CostEstimate(flops=4_000_000_000, bytes_accessed=12_000_000, transcendentals=4_000_000),
+        compiler_params=pltpu.CompilerParams(vmem_limit_bytes=44 * 1024 * 1024),
         name="front",
-    )(scalars, kept, got, kept, got, kept, conv_weight, bias_row, conv_weight, bias_row, dt_row, decay_row)
+    )(scalars, kept, got, conv_weight, bias_row, conv_weight, bias_row, dt_row, decay_row)
 
     received = lax.all_to_all(payload, SEQ, 0, 0, tiled=True)
     block_tile = lambda columns, index: pl.BlockSpec((BLOCK, columns), index)
@@ -478,6 +478,7 @@
         out_shape=jax.ShapeDtypeStruct((count, chunk_rows, state_width), F32),
         scratch_shapes=[pltpu.VMEM((state_width, count), F32)],
         cost_estimate=pl.CostEstimate(flops=2_000_000_000, bytes_accessed=3_000_000, transcendentals=0),
+        compiler_params=pltpu.CompilerParams(vmem_limit_bytes=10 * 1024 * 1024),
         name="prefix",
     )(lax.axis_index(SEQ).astype(jnp.int32)[None], received)
     weight, _ = lax.optimization_barrier((weight, before))
@@ -497,7 +498,7 @@
             block_tile(inner, lambda q: (q, 0)),
             block_tile(state_width, lambda q: (q, 1)),
             block_tile(state_width, lambda q: (q, 0)),
-            whole((inner, state_width)),
+            pl.BlockSpec(memory_space=pltpu.VMEM),
             whole((1, inner)),
         ],
         out_specs=block_tile(inner, lambda q: (q, 0)),

time: 249 us -> 244 us (0.980)
    unnamed x14 -> x24, local copies, waits for them, and re-layouts: 6.23 us -> 5.87 us
  transfers between devices with their start and end apart: 8 -> 8, of which waited for: 6 -> 6; matrix products, arithmetic and copies ran while one was open for 7% -> 6% of each run, Pallas kernels for 13% -> 13%
where the time goes in v4:
time: 244 us; the launch traced here: 243 us
  waiting for transfers between devices  105 us (43%)
  Pallas kernels  70.8 us (29%)
  matrix products  19.8 us (8%)
  starting transfers between devices  19.7 us (8%)
  between operations  14.7 us (6%)
  local copies, waits for them, and re-layouts  8.64 us (4%)
  other arithmetic  4.22 us (2%)
    all_gather x1, waiting for transfers between devices, local(): weight = lax.all_gather(shard, SEQ, axis=0, tiled=True)  79.6 us
    pallas_call x1, Pallas kernels, local(): pl.pallas_call(functools.partial(inner_kernel, head_dim, heads), grid=(ca...  22.4 us
    pallas_call x2, Pallas kernels, project(): pl.pallas_call(project_kernel, grid=(count // tile,), in_specs=[pl.BlockS...  19.8 us
    dot_general x2, matrix products, projected(): return jnp.dot(rows, part, preferred_element_type=F32).astype(BF16)  19.8 us
    pallas_call x1, Pallas kernels, local(): pl.pallas_call(functools.partial(front_kernel, heads, head_dim, chunk_row...  13.7 us
    all_to_all x1, waiting for transfers between devices, local(): lax.all_to_all(before, SEQ, 0, 0, tiled=True).reshape(inner, state_width)  12.5 us
    pallas_call x1, Pallas kernels, local(): pl.pallas_call(functools.partial(finish_kernel, head_dim), grid=(capacity...  11.6 us
    all_to_all x1, starting transfers between devices, local(): received = lax.all_to_all(payload, SEQ, 0, 0, tiled=True)  8.78 us
  transfers between devices with their start and end apart: 8, of which 6 were waited for; matrix products, arithmetic and copies ran while one was open for 6% of the time, Pallas kernels for 13%

profile of v4, /device:TPU:0, one launch (start us, length us, event | category | flops | bytes accessed | tf_op | source)
XLA Modules:
  0.0 243.0 jit_solution(4630738642464333727)
XLA Ops:
  6.5 0.0 all-gather.2.cloned.1.call-start
  6.5 1.7 pack.1
  8.2 0.0 collective-permute-start.1
  8.2 1.6 collective-permute-done.1
  9.8 1.8 maximum_select_fusion
  11.5 0.0 all-gather.2.cloned.1.call-update
  11.6 1.4 fusion.10
  14.2 0.8 dynamic-slice_bitcast_fusion
  14.9 3.5 %collective-permute-start = (bf16[8,2560]{1,0:T(8,128)(2,1)S(1)}, bf16[8,2560]{1,0:T(8,128)(2,1)S(1)}, u32[]{:S(2)}, u32[]{:S(2)}) collective-permute-start(bf16[8,2560]{1,0:T(8,128)(2,1)S(1)} %dynamic-slice_bitcast_fusion), channel_id=1, source_target_pairs={{0,2},{2,4},{4,6},{6,8},{8,10},{10,12},{12,14},{14,16},{16,18},{18... | collective-permute-start | bytes 122888 | tf_op jit(solution)/shard_map/ppermute | solution.py:23
  18.4 1.7 collective-permute-done
  20.1 2.4 pad_maximum_fusion.rows_ref
  22.5 0.0 copy-start.7
  22.5 2.0 copy-done.7
  24.4 0.0 copy-start.11
  24.4 0.0 copy-start.10
  24.4 0.0 collective-permute-start.2
  24.4 7.0 %collective-permute-done.2.rows_ref = bf16[776,2560]{1,0:T(8,128)(2,1)} collective-permute-done((bf16[776,2560]{1,0:T(8,128)(2,1)S(1)}, bf16[776,2560]{1,0:T(8,128)(2,1)}, u32[]{:S(2)}, u32[]{:S(2)}) %collective-permute-start.2) | collective-permute-done | bytes 3973152 | tf_op jit(solution)/shard_map/ppermute | solution.py:27
  31.4 79.6 %all-gather.2.cloned.1.call-done.weight_ref = bf16[2560,2816]{1,0:T(8,128)(2,1)} async-done(((bf16[40,2816]{1,0:T(8,128)(2,1)}), bf16[2560,2816]{1,0:T(8,128)(2,1)}) %all-gather.2.cloned.1.call-update) | async-done | bytes 14417936 | tf_op jit(solution)/shard_map/all_gather | solution.py:376
  111.0 9.9 %fusion.7 = bf16[776,1536]{1,0:T(8,128)(2,1)S(1)} fusion(bf16[776,2560]{1,0:T(8,128)(2,1)} %collective-permute-done.2.rows_ref, bf16[2560,2816]{1,0:T(8,128)(2,1)} %all-gather.2.cloned.1.call-done.weight_ref), kind=kOutput, calls=%fused_computation.6 | convolution fusion | flops 6103904256 | bytes 14221312 | tf_op jit(solution)/shard_map/dot_general | solution.py:385
  120.9 0.1 collective-permute-start.3
  121.0 0.0 copy-done.11
  121.0 0.6 broadcast_in_dim.23.gain_ref
  121.6 0.0 copy-done.10
  121.6 0.1 pad_add_fusion.scalars
  121.7 0.0 copy-start.2
  121.7 9.9 %fusion.4.kept_ref = bf16[776,1536]{1,0:T(8,128)(2,1)S(1)} fusion(bf16[776,2560]{1,0:T(8,128)(2,1)} %copy-done.7, bf16[2560,2816]{1,0:T(8,128)(2,1)} %all-gather.2.cloned.1.call-done.weight_ref), kind=kOutput, calls=%fused_computation.5 | convolution fusion | flops 6103904256 | bytes 14221312 | tf_op jit(solution)/shard_map/dot_general | solution.py:385
  131.7 0.0 collective-permute-done.3.got_ref
  131.7 0.0 copy-done.2
  131.7 0.0 copy-done.3
  131.7 0.0 copy-done.4
  131.7 0.0 copy-done.5
  131.7 13.7 %front.1 = (bf16[768,2560]{1,0:T(8,128)(2,1)}, bf16[768,256]{1,0:T(8,128)(2,1)S(1)}, f32[768,128]{1,0:T(8,128)S(1)}, f32[768,128]{1,0:T(8,128)S(1)}, f32[64,48,128]{2,1,0:T(8,128)}) custom-call(s32[2]{0:T(128)S(1)} %pad_add_fusion.scalars, bf16[776,1536]{1,0:T(8,128)(2,1)S(1)} %fusion.4.kept_ref, bf16[776,1536]{1,0:T(8,128)(2,1)} %collective-permute-done.3.got_ref, ...), custom_call_target="tpu_custom_call" | custom-call | flops 4000000000 | bytes 12000000 | tf_op jit(solution)/shard_map/front/pallas_call | solution.py:406
  145.4 0.7 copy-done
  146.1 0.7 copy-done.1
  146.9 0.7 copy-done.6
  147.6 8.8 %all-to-all-start = ((f32[64,48,128]{2,1,0:T(8,128)}), f32[64,48,128]{2,1,0:T(8,128)S(1)}, u32[]{:S(2)}, u32[]{:S(2)}) async-start(f32[64,48,128]{2,1,0:T(8,128)} %get-tuple-element.24), calls=%async_computation | async-start | bytes 3145728 | tf_op jit(solution)/shard_map/all_to_all | solution.py:448
  156.4 22.4 %inner.1.y_ref = f32[768,2560]{1,0:T(8,128)} custom-call(s32[2]{0:T(128)} %copy-done.2, bf16[768,2560]{1,0:T(8,128)(2,1)} %get-tuple-element.25.x_ref, bf16[768,256]{1,0:T(8,128)(2,1)} %copy-done, f32[768,128]{1,0:T(8,128)} %copy-done.1, f32[768,128]{1,0:T(8,128)} %copy-done.6, f32[1,40]{1,0:T(1,128)} %bitcast.19), custom_call_target="tpu_custom_call" | custom-call | flops 20000000000 | bytes 14000000 | tf_op jit(solution)/shard_map/inner/pallas_call | solution.py:450
  178.8 2.8 %all-to-all-done.got_ref = f32[64,48,128]{2,1,0:T(8,128)S(1)} async-done(((f32[64,48,128]{2,1,0:T(8,128)}), f32[64,48,128]{2,1,0:T(8,128)S(1)}, u32[]{:S(2)}, u32[]{:S(2)}) %all-to-all-start) | async-done | bytes 1572896 | tf_op jit(solution)/shard_map/all_to_all | solution.py:448
  181.6 1.7 prefix.1
  183.3 9.9 %project_gate.3 = bf16[776,1280]{1,0:T(8,128)(2,1)} custom-call(bf16[776,2560]{1,0:T(8,128)(2,1)} %collective-permute-done.2.rows_ref, bf16[2560,2816]{1,0:T(8,128)(2,1)} %all-gather.2.cloned.1.call-done.weight_ref), custom_call_target="tpu_custom_call" | custom-call | flops 5085593600 | bytes 14000000 | tf_op jit(solution)/shard_map/project_gate/pallas_call | solution.py:49
  193.1 0.0 collective-permute-start.4
  193.2 7.4 %all-to-all-start.1 = ((f32[64,40,128]{2,1,0:T(8,128)}), f32[64,40,128]{2,1,0:T(8,128)S(1)}, u32[]{:S(2)}, u32[]{:S(2)}) async-start(f32[64,40,128]{2,1,0:T(8,128)} %prefix.1), calls=%async_computation.1 | async-start | bytes 2621440 | tf_op jit(solution)/shard_map/all_to_all | solution.py:489
  200.5 9.9 %project_gate.2.kept_ref = bf16[776,1280]{1,0:T(8,128)(2,1)} custom-call(bf16[776,2560]{1,0:T(8,128)(2,1)} %copy-done.7, bf16[2560,2816]{1,0:T(8,128)(2,1)} %all-gather.2.cloned.1.call-done.weight_ref), custom_call_target="tpu_custom_call" | custom-call | flops 5085593600 | bytes 14000000 | tf_op jit(solution)/shard_map/project_gate/pallas_call | solution.py:49
  210.4 12.5 %all-to-all-done.1 = f32[64,40,128]{2,1,0:T(8,128)S(1)} async-done(((f32[64,40,128]{2,1,0:T(8,128)}), f32[64,40,128]{2,1,0:T(8,128)S(1)}, u32[]{:S(2)}, u32[]{:S(2)}) %all-to-all-start.1) | async-done | bytes 1310752 | tf_op jit(solution)/shard_map/all_to_all | solution.py:489
  222.9 0.0 collective-permute-done.4.got_ref
  222.9 1.2 copy-done.8
  224.1 0.5 copy-done.9
  224.6 11.6 %finish.1 = bf16[768,2560]{1,0:T(8,128)(2,1)} custom-call(s32[2]{0:T(128)} %copy-done.2, bf16[776,1280]{1,0:T(8,128)(2,1)} %project_gate.2.kept_ref, bf16[776,1280]{1,0:T(8,128)(2,1)} %copy-done.9, f32[768,2560]{1,0:T(8,128)} %inner.1.y_ref, bf16[768,256]{1,0:T(8,128)(2,1)} %copy-done, f32[768,128]{1,0:T(8,128)} %copy-done.1, f32[2560,128]{1,0:T(8,128)} %bitcast.17, ...), custom_call_target="tpu_custom_call" | custom-call | flops 4000000000 | bytes 18000000 | tf_op jit(solution)/shard_map/finish/pallas_call | solution.py:491
  (9 shorter events, 0.0 us)
Async XLA Ops:
  6.5 104.5 %all-gather.2.cloned.1.call-start = ((), (), s32[]{:S(2)}) async-start(), calls=%async_computation.2 | async-start | bytes 14643200 | tf_op jit(solution)/shard_map/all_gather | solution.py:376
  8.2 1.6 collective-permute-start.1
  14.9 5.2 %collective-permute-start = (bf16[8,2560]{1,0:T(8,128)(2,1)S(1)}, bf16[8,2560]{1,0:T(8,128)(2,1)S(1)}, u32[]{:S(2)}, u32[]{:S(2)}) collective-permute-start(bf16[8,2560]{1,0:T(8,128)(2,1)S(1)} %dynamic-slice_bitcast_fusion), channel_id=1, source_target_pairs={{0,2},{2,4},{4,6},{6,8},{8,10},{10,12},{12,14},{14,16},{16,18},{18... | collective-permute-start | bytes 122888 | tf_op jit(solution)/shard_map/ppermute | solution.py:23
  22.5 2.0 copy-start.7
  24.4 96.6 %copy-start.11 = (f32[2560]{0:T(1024)S(1)}, f32[2560]{0:T(1024)}, u32[]{:S(2)}) copy-start(f32[2560]{0:T(1024)} %param.17) | copy-start | bytes 30724
  24.4 97.2 %copy-start.10 = (f32[2816]{0:T(1024)S(1)}, f32[2816]{0:T(1024)}, u32[]{:S(2)}) copy-start(f32[2816]{0:T(1024)} %param.13) | copy-start | bytes 33796
  24.4 7.0 %collective-permute-start.2 = (bf16[776,2560]{1,0:T(8,128)(2,1)S(1)}, bf16[776,2560]{1,0:T(8,128)(2,1)}, u32[]{:S(2)}, u32[]{:S(2)}) collective-permute-start(bf16[776,2560]{1,0:T(8,128)(2,1)S(1)} %pad_maximum_fusion.rows_ref), channel_id=1, source_target_pairs={{0,1},{1,0},{2,3},{3,2},{4,5},{5,4},{6,7},{7,6},{8,9},{9,8},{10,11... | collective-permute-start | bytes 11919368 | tf_op jit(solution)/shard_map/ppermute | solution.py:27
  120.9 10.8 %collective-permute-start.3 = (bf16[776,1536]{1,0:T(8,128)(2,1)S(1)}, bf16[776,1536]{1,0:T(8,128)(2,1)}, u32[]{:S(2)}, u32[]{:S(2)}) collective-permute-start(bf16[776,1536]{1,0:T(8,128)(2,1)S(1)} %fusion.7), channel_id=1, source_target_pairs={{0,1},{1,0},{2,3},{3,2},{4,5},{5,4},{6,7},{7,6},{8,9},{9,8},{10,11... | collective-permute-start | bytes 7151624 | tf_op jit(solution)/shard_map/ppermute | solution.py:27
  121.7 9.9 %copy-start.2 = (s32[2]{0:T(128)}, s32[2]{0:T(128)S(1)}, u32[]{:S(2)}) copy-start(s32[2]{0:T(128)S(1)} %pad_add_fusion.scalars) | copy-start | bytes 28
  121.7 10.0 %copy-start.3 = (f32[4,2816]{1,0:T(4,128)S(1)}, f32[4,2816]{1,0:T(4,128)}, u32[]{:S(2)}) copy-start(f32[4,2816]{1,0:T(4,128)} %map_conv_ref.1) | copy-start | bytes 135172
  121.7 10.0 %copy-start.4 = (f32[40]{0:T(128)S(1)}, f32[40]{0:T(128)}, u32[]{:S(2)}) copy-start(f32[40]{0:T(128)} %param.14) | copy-start | bytes 484
  121.7 10.0 %copy-start.5 = (f32[40]{0:T(128)S(1)}, f32[40]{0:T(128)}, u32[]{:S(2)}) copy-start(f32[40]{0:T(128)} %param.15) | copy-start | bytes 484
  145.4 0.7 copy-start
  146.1 0.7 copy-start.1
  146.9 0.7 copy-start.6
  147.6 34.0 %all-to-all-start = ((f32[64,48,128]{2,1,0:T(8,128)}), f32[64,48,128]{2,1,0:T(8,128)S(1)}, u32[]{:S(2)}, u32[]{:S(2)}) async-start(f32[64,48,128]{2,1,0:T(8,128)} %get-tuple-element.24), calls=%async_computation | async-start | bytes 3145728 | tf_op jit(solution)/shard_map/all_to_all | solution.py:448
  193.1 29.8 %collective-permute-start.4 = (bf16[776,1280]{1,0:T(8,128)(2,1)}, bf16[776,1280]{1,0:T(8,128)(2,1)S(1)}, u32[]{:S(2)}, u32[]{:S(2)}) collective-permute-start(bf16[776,1280]{1,0:T(8,128)(2,1)} %project_gate.3), channel_id=1, source_target_pairs={{0,1},{1,0},{2,3},{3,2},{4,5},{5,4},{6,7},{7,6},{8,9},{9,8},{10,11... | collective-permute-start | bytes 5959688 | tf_op jit(solution)/shard_map/ppermute | solution.py:27
  193.2 29.8 %all-to-all-start.1 = ((f32[64,40,128]{2,1,0:T(8,128)}), f32[64,40,128]{2,1,0:T(8,128)S(1)}, u32[]{:S(2)}, u32[]{:S(2)}) async-start(f32[64,40,128]{2,1,0:T(8,128)} %prefix.1), calls=%async_computation.1 | async-start | bytes 2621440 | tf_op jit(solution)/shard_map/all_to_all | solution.py:489
  222.9 1.2 copy-start.8
  222.9 1.7 copy-start.9
Sparse Core Ops, SparseCore 0:
  11.7 99.2 all-gather.1
